TPU v7x, 128 devices: a whole 4x4x4 slice. The times are simulated.
128 devices in a mesh: row: 8 (over z, y_hi), col: 16 (over x, y_lo, core).
Axes of the slice: x: 4, y: 4 (y_hi: 2, y_lo: 2; y = y_hi * 2 + y_lo), z: 4, core: 2. Of those that a mesh axis runs over, the one named last changes fastest.
Arguments:
- atom_y: float32 [65536], P('col'), may hold values from 0 to 1024, as said below
- atom_x: float32 [65536], P('col'), may hold values from 0 to 1024
- atom_weight: float32 [65536], P('col'), may hold values from 0.5 to 2
- beam_ky: int32 [128], replicated, may hold values from -16 to 16
- beam_kx: int32 [128], replicated, may hold values from -16 to 16
- beam_amplitude: float32 [128], replicated, may hold values from 0.2 to 1.8
- crop_offset: int32 [2], replicated, may hold values from 0 to 512
- probe_y: int32 [8, 16, 128], P('row', 'col'), may hold values from 0 to 511
- probe_x: int32 [8, 16, 128], P('row', 'col'), may hold values from 0 to 511
Outputs:
- intensity: float32 [8, 16, 128, 2048], P('row', 'col')
Inputs may be any that keep to these rules, and one draw needn't show every extreme that they name: Rows are grouped in bands of 16; atom i of each atom block (counted from the block's first atom) lies in band i // 64, that is 16 * band <= atom_y < 16 * band + 16.
All inputs are finite; a program needn't handle non-finite values.
Results may differ from a plain program's by a relative error of at most 0.012.
Values may be sent and summed in bfloat16 or wider, within the bound.
A program may use at most 64 MiB of HBM per device.

v0:
```python
import math

import jax
import jax.numpy as jnp
from jax import lax
from jax.sharding import PartitionSpec as P

N = 1024
WIN = 512


interaction = 1.0
gauss_width = 2.0
two_pi = 2.0 * math.pi


def total_of_pieces(value, axis):
    pieces = lax.all_gather(value, axis).astype(jnp.float32)
    return pieces.sum(axis=0)


def unit_phase(integer_phase, modulus, factor):
    angle = two_pi / modulus * jnp.mod(integer_phase, modulus).astype(jnp.float32)
    return (jnp.cos(angle) * factor, jnp.sin(angle) * factor)


def complex_dot(left_re, left_im, right_re, right_im):
    height = left_re.shape[0]
    across = right_re.shape[1]
    stacked = jnp.dot(
        jnp.concatenate([left_re, left_im], 0),
        jnp.concatenate([right_re, right_im], 1),
        preferred_element_type=jnp.float32,
    )
    real = stacked[:height, :across] - stacked[height:, across:]
    imag = stacked[:height, across:] + stacked[height:, :across]
    return (real, imag)


def body(
    atom_y, atom_x, atom_weight, beam_ky, beam_kx, beam_amplitude, crop_offset, probe_y, probe_x
):
    row_count = lax.axis_size("row")
    col_count = lax.axis_size("col")
    row_place = lax.axis_index("row")
    col_place = lax.axis_index("col")
    block_rows = N // row_count
    row_start = (row_place * block_rows).astype(jnp.float32)
    places_y = row_start + jnp.arange(block_rows).astype(jnp.float32)
    places_x = jnp.arange(N).astype(jnp.float32)
    profile_y = jnp.exp(-jnp.square((places_y[None, :] - atom_y[:, None]) / gauss_width))
    profile_x = (
        jnp.exp(-jnp.square((places_x[None, :] - atom_x[:, None]) / gauss_width))
        * atom_weight[:, None]
    )
    partial_value = lax.dot_general(
        profile_y, profile_x, (((0,), (0,)), ((), ())), preferred_element_type=jnp.float32
    )
    band = total_of_pieces(partial_value.astype(jnp.bfloat16), "col").astype(jnp.float32)
    potential = lax.all_gather(band.astype(jnp.bfloat16), "row", axis=0, tiled=True).astype(
        band.dtype
    )
    index = jnp.arange(N, dtype=jnp.int32)
    forward_re, forward_im = unit_phase(-index[:, None] * index[None, :], N, 1.0)
    forward_re = forward_re.astype(jnp.bfloat16)
    forward_im = forward_im.astype(jnp.bfloat16)
    signed = jnp.where(index < N // 2, index, index - N)
    square = signed * signed
    prop_re, prop_im = unit_phase(-(square[:, None] + square[None, :]), 4 * N, 1.0)
    window = jnp.arange(WIN, dtype=jnp.int32)
    back_yre, back_yim = unit_phase((crop_offset[0] + window)[:, None] * index[None, :], N, 1.0 / N)
    back_xre, back_xim = unit_phase(index[:, None] * (crop_offset[1] + window)[None, :], N, 1.0 / N)
    beam_number = row_place * col_count + col_place
    freq_y = lax.dynamic_index_in_dim(beam_ky, beam_number, keepdims=False)
    freq_x = lax.dynamic_index_in_dim(beam_kx, beam_number, keepdims=False)
    beam_phase = jnp.mod(freq_y * index[:, None] + freq_x * index[None, :], N)
    angle = interaction * potential + two_pi / N * beam_phase.astype(jnp.float32)
    wave_re = jnp.cos(angle).astype(jnp.bfloat16)
    wave_im = jnp.sin(angle).astype(jnp.bfloat16)
    first_re, first_im = complex_dot(forward_re, forward_im, wave_re, wave_im)
    second_re, second_im = complex_dot(
        first_re.astype(jnp.bfloat16), first_im.astype(jnp.bfloat16), forward_re, forward_im
    )
    moved_re = (second_re * prop_re - second_im * prop_im).astype(jnp.bfloat16)
    moved_im = (second_re * prop_im + second_im * prop_re).astype(jnp.bfloat16)
    third_re, third_im = complex_dot(
        back_yre.astype(jnp.bfloat16), back_yim.astype(jnp.bfloat16), moved_re, moved_im
    )
    final_re, final_im = complex_dot(
        third_re.astype(jnp.bfloat16),
        third_im.astype(jnp.bfloat16),
        back_xre.astype(jnp.bfloat16),
        back_xim.astype(jnp.bfloat16),
    )
    field = jnp.stack([final_re.astype(jnp.bfloat16), final_im.astype(jnp.bfloat16)])
    tile_rows = WIN // row_count
    tile_cols = WIN // col_count
    outgoing = field.reshape(2, row_count, tile_rows, col_count, tile_cols).transpose(0, 1, 3, 2, 4)
    sectioned = lax.all_to_all(
        lax.all_to_all(
            outgoing.reshape(2, row_count, col_count, tile_rows * tile_cols),
            "col",
            split_axis=2,
            concat_axis=2,
            tiled=True,
        ),
        "row",
        split_axis=1,
        concat_axis=1,
        tiled=True,
    )
    incoming = sectioned.reshape(2, row_count * col_count, tile_rows * tile_cols)
    beam_total = row_count * col_count
    weights = beam_amplitude / math.sqrt(beam_total)
    where_y = probe_y[0, 0]
    where_x = probe_x[0, 0]
    integer = beam_ky[None, :] * (where_y[:, None] + crop_offset[0]) + beam_kx[None, :] * (
        where_x[:, None] + crop_offset[1]
    )
    coeff_re, coeff_im = unit_phase(-integer, N, 1.0)
    coeff_re = (coeff_re * weights[None, :]).astype(jnp.bfloat16)
    coeff_im = (coeff_im * weights[None, :]).astype(jnp.bfloat16)
    probe_re, probe_im = complex_dot(coeff_re, coeff_im, incoming[0], incoming[1])
    result = jnp.square(probe_re) + jnp.square(probe_im)
    return result[None, None]


def solution(mesh):
    return jax.shard_map(
        body,
        mesh=mesh,
        in_specs=(
            P("col"),
            P("col"),
            P("col"),
            P(),
            P(),
            P(),
            P(),
            P("row", "col", None),
            P("row", "col", None),
        ),
        out_specs=P("row", "col", None, None),
        check_vma=False,
    )
```

profile of v0, /device:TPU:0, one launch (start us, length us, event | category | flops | bytes accessed | tf_op | source)
XLA Modules:
  0.0 259.8 jit_solution(12487123532036467879)
XLA Ops:
  6.5 6.6 %fusion.78 = bf16[128,1024]{1,0:T(8,128)(2,1)} fusion(f32[4096]{0:T(1024)} %param.11, f32[4096]{0:T(1024)} %param.10, f32[1024]{0:T(1024)S(1)} %iota_convert_fusion, f32[4096]{0:T(1024)} %param.9, f32[128]{0:T(128)S(1)} %convert_add_fusion), kind=kOutput, calls=%fused_computation.113 | convolution fusion | flops 1096941568 | bytes 315904 | tf_op jit(solution)/shard_map/dot_general | solution.py:56
  13.1 0.0 all-gather.6.cloned.1.call-update
  13.2 0.0 all-gather.4.cloned.1.call-start
  13.2 39.8 %all-gather.6.cloned.1.call-done = bf16[2048,1024]{1,0:T(8,128)(2,1)} async-done(((bf16[128,1024]{1,0:T(8,128)(2,1)}), bf16[2048,1024]{1,0:T(8,128)(2,1)}) %all-gather.6.cloned.1.call-update) | async-done | bytes 4194320 | tf_op jit(solution)/shard_map/all_gather | solution.py:18
  53.0 3.1 %reduce_sum.12 = bf16[128,1024]{1,0:T(8,128)(2,1)S(1)} reduce(bf16[16,128,1024]{2,1,0:T(8,128)(2,1)} %bitcast.23, bf16[]{:T(256)} %constant.92.clone.1), dimensions={0}, to_apply=%region_0.0 | reduce | flops 1966080 | bytes 4456450 | tf_op jit(solution)/shard_map/reduce_sum | solution.py:19
  56.1 0.8 copy.13
  57.0 0.0 all-gather.4.cloned.1.call-update
  57.0 0.6 dynamic_slice.7
  57.6 0.6 dynamic_slice.8
  58.2 0.6 fusion.110
  58.8 0.7 iota_add_fusion.1
  59.5 0.6 iota_add_fusion
  60.1 1.3 iota_multiply_fusion
  61.4 9.6 %multiply_convert_fusion.1 = (bf16[1024,512]{1,0:T(8,128)(2,1)S(1)}, bf16[1024,512]{1,0:T(8,128)(2,1)}) fusion(s32[512]{0:T(512)S(1)} %iota_add_fusion), kind=kLoop, calls=%fused_computation.97 | loop fusion | flops 9437184 | bytes 2099200 | tf_op jit(solution)/shard_map/convert_element_type | solution.py:92
  71.0 10.5 %multiply_convert_fusion.3 = (bf16[512,1024]{1,0:T(8,128)(2,1)}, bf16[512,1024]{1,0:T(8,128)(2,1)}) fusion(s32[512]{0:T(512)S(1)} %iota_add_fusion.1), kind=kLoop, calls=%fused_computation.108 | loop fusion | flops 9437184 | bytes 2099200 | tf_op jit(solution)/shard_map/convert_element_type | solution.py:87
  81.5 18.0 %cosine_convert_fusion.1 = (bf16[1024,1024]{0,1:T(8,128)(2,1)S(1)}, bf16[1024,1024]{0,1:T(8,128)(2,1)}) fusion(s32[1024]{0:T(1024)S(1)} %iota_negate_fusion), kind=kLoop, calls=%fused_computation.64 | loop fusion | flops 16777216 | bytes 4198400 | tf_op jit(solution)/shard_map/convert_element_type | solution.py:65
  99.5 12.1 %all-gather.4.cloned.1.call-done = bf16[1024,1024]{0,1:T(8,128)(2,1)} async-done(((bf16[128,1024]{0,1:T(8,128)(2,1)}), bf16[1024,1024]{0,1:T(8,128)(2,1)}) %all-gather.4.cloned.1.call-update) | async-done | bytes 2097168 | tf_op jit(solution)/shard_map/all_gather | solution.py:60
  111.6 19.4 %cosine_convert_fusion = (bf16[1024,1024]{0,1:T(8,128)(2,1)S(1)}, bf16[1024,1024]{0,1:T(8,128)(2,1)S(1)}) fusion(s32[1024]{0:T(1024)S(1)} %get-tuple-element.27, s32[1024]{0:T(1024)S(1)} %get-tuple-element.28, bf16[1024,1024]{0,1:T(8,128)(2,1)} %all-gather.4.cloned.1.call-done), kind=kLoop, calls=%fused_computation.62 | loop fusion | flops 18874368 | bytes 6299648 | tf_op jit(solution)/shard_map/convert_element_type | solution.py:78
  131.0 13.8 %fusion.25 = f32[2048,2048]{1,0:T(8,128)} fusion(bf16[1024,1024]{0,1:T(8,128)(2,1)S(1)} %copy-done, bf16[1024,1024]{0,1:T(8,128)(2,1)S(1)} %get-tuple-element.17, bf16[1024,1024]{0,1:T(8,128)(2,1)S(1)} %get-tuple-element.14, bf16[1024,1024]{0,1:T(8,128)(2,1)S(1)} %get-tuple-element.13), kind=kOutput, calls=%fused_computation.41 | convolution fusion | flops 8606711808 | bytes 25165824 | tf_op jit(solution)/shard_map/dot_general | solution.py:30
  144.8 6.6 %fusion.24 = (bf16[1024,1024]{1,0:T(8,128)(2,1)S(1)}, bf16[1024,1024]{1,0:T(8,128)(2,1)S(1)}) fusion(f32[2048,2048]{1,0:T(8,128)} %fusion.25), kind=kLoop, calls=%fused_computation.40 | loop fusion | flops 4194304 | bytes 20971520 | tf_op jit(solution)/shard_map/convert_element_type | solution.py:82
  151.4 13.5 %fusion.32 = f32[2048,2048]{0,1:T(8,128)} fusion(bf16[1024,1024]{1,0:T(8,128)(2,1)S(1)} %get-tuple-element.8, bf16[1024,1024]{1,0:T(8,128)(2,1)S(1)} %get-tuple-element.7, bf16[1024,1024]{0,1:T(8,128)(2,1)S(1)} %copy-done, bf16[1024,1024]{0,1:T(8,128)(2,1)S(1)} %get-tuple-element.17), kind=kOutput, calls=%fused_computation.48 | convolution fusion | flops 8606711808 | bytes 25165824 | tf_op jit(solution)/shard_map/dot_general | solution.py:30
  164.9 21.0 %subtract_convert_fusion = (bf16[1024,1024]{0,1:T(8,128)(2,1)S(1)}, bf16[1024,1024]{0,1:T(8,128)(2,1)S(1)}) fusion(s32[1024]{0:T(1024)S(1)} %fusion.102, f32[2048,2048]{0,1:T(8,128)} %fusion.32), kind=kLoop, calls=%fused_computation.60 | loop fusion | flops 25165824 | bytes 20979712 | tf_op jit(solution)/shard_map/convert_element_type | solution.py:84
  185.9 4.6 %fusion.39 = f32[1024,2048]{1,0:T(8,128)S(1)} fusion(bf16[1024,1024]{0,1:T(8,128)(2,1)S(1)} %get-tuple-element.6, bf16[1024,1024]{0,1:T(8,128)(2,1)S(1)} %get-tuple-element.5, bf16[512,1024]{1,0:T(8,128)(2,1)S(1)} %copy-done.3, bf16[512,1024]{1,0:T(8,128)(2,1)S(1)} %copy-done.2), kind=kOutput, calls=%fused_computation.55 | convolution fusion | flops 4307550208 | bytes 14680064 | tf_op jit(solution)/shard_map/dot_general | solution.py:30
  190.4 0.0 copy-start.1
  190.4 0.8 fusion.54
  191.2 0.5 copy-done.1
  191.6 2.3 fusion.58
  194.0 0.4 fusion.88
  194.3 0.2 copy.15
  194.6 0.5 stack.10
  195.1 0.2 copy.14
  195.3 1.5 stack.9
  196.8 1.7 maximum_bitcast_fusion
  198.5 3.3 %copy.19 = bf16[2,8,16,64,32]{4,3,1,0,2:T(8,128)(2,1)} copy(bf16[2,8,16,64,32]{3,1,4,2,0:T(8,128)(2,1)S(1)} %maximum_bitcast_fusion) | data formatting | bytes 2097152 | tf_op jit(solution)/shard_map/reshape | solution.py:101
  201.8 6.0 %reshape.89 = bf16[2,8,16,2048]{3,1,0,2:T(8,128)(2,1)S(1)} reshape(bf16[2,8,16,64,32]{4,3,1,0,2:T(8,128)(2,1)} %copy.19) | data formatting | bytes 2097152 | tf_op jit(solution)/shard_map/reshape | solution.py:101
  207.8 0.0 copy-start.9
  207.8 0.0 copy-start.7
  207.8 0.0 copy-start.8
  207.8 20.8 %all_to_all.10 = bf16[2,8,16,2048]{3,1,0,2:T(8,128)(2,1)S(1)} all-to-all(bf16[2,8,16,2048]{3,1,0,2:T(8,128)(2,1)S(1)} %reshape.89), channel_id=1, replica_groups=mesh['row'=8,'col'=16] {'col'}, dimensions={2} | all-to-all | bytes 2097152 | tf_op jit(solution)/shard_map/all_to_all | solution.py:100
  228.6 1.5 copy.18
  230.1 4.1 %all-to-all-start.1 = ((bf16[2,8,16,2048]{3,2,0,1:T(8,128)(2,1)}), bf16[2,8,16,2048]{3,2,0,1:T(8,128)(2,1)S(1)}, u32[]{:S(2)}, u32[]{:S(2)}) async-start(bf16[2,8,16,2048]{3,2,0,1:T(8,128)(2,1)} %copy.18), calls=%async_computation.1 | async-start | bytes 2097152 | tf_op jit(solution)/shard_map/all_to_all | solution.py:99
  234.3 0.0 copy-done.9
  234.3 1.3 add_bitcast_fusion
  235.6 0.4 multiply_convert_fusion.5
  236.0 14.9 %all-to-all-done.1 = bf16[2,8,16,2048]{3,2,0,1:T(8,128)(2,1)S(1)} async-done(((bf16[2,8,16,2048]{3,2,0,1:T(8,128)(2,1)}), bf16[2,8,16,2048]{3,2,0,1:T(8,128)(2,1)S(1)}, u32[]{:S(2)}, u32[]{:S(2)}) %all-to-all-start.1) | async-done | bytes 1048608 | tf_op jit(solution)/shard_map/all_to_all | solution.py:99
  250.9 0.1 fusion.109
  251.0 0.7 fusion.89
  251.7 1.3 fusion.85
  (20 shorter events, 0.0 us)
Async XLA Ops:
  6.5 46.5 %all-gather.6.cloned.1.call-start = ((), (), s32[]{:S(2)}) async-start(), calls=%async_computation.3 | async-start | bytes 4456448 | tf_op jit(solution)/shard_map/all_gather | solution.py:18
  13.1 43.9 %copy-start.6 = (s32[128]{0:T(128)S(1)}, s32[128]{0:T(128)}, u32[]{:S(2)}) copy-start(s32[128]{0:T(128)} %param.12) | copy-start | bytes 1540
  13.1 44.5 %copy-start.5 = (s32[128]{0:T(128)S(1)}, s32[128]{0:T(128)}, u32[]{:S(2)}) copy-start(s32[128]{0:T(128)} %param.13) | copy-start | bytes 1540
  13.1 45.0 %copy-start.4 = (s32[2]{0:T(128)S(1)}, s32[2]{0:T(128)}, u32[]{:S(2)}) copy-start(s32[2]{0:T(128)} %param.15) | copy-start | bytes 28
  13.2 98.4 %all-gather.4.cloned.1.call-start = ((), (), s32[]{:S(2)}) async-start(), calls=%async_computation.2 | async-start | bytes 2359296 | tf_op jit(solution)/shard_map/all_gather | solution.py:60
  111.6 19.4 %copy-start = (bf16[1024,1024]{0,1:T(8,128)(2,1)S(1)}, bf16[1024,1024]{0,1:T(8,128)(2,1)}, u32[]{:S(2)}) copy-start(bf16[1024,1024]{0,1:T(8,128)(2,1)} %get-tuple-element.18) | copy-start | bytes 6291460
  164.9 21.0 %copy-start.2 = (bf16[512,1024]{1,0:T(8,128)(2,1)S(1)}, bf16[512,1024]{1,0:T(8,128)(2,1)}, u32[]{:S(2)}) copy-start(bf16[512,1024]{1,0:T(8,128)(2,1)} %get-tuple-element.23) | copy-start | bytes 3145732
  164.9 21.0 %copy-start.3 = (bf16[512,1024]{1,0:T(8,128)(2,1)S(1)}, bf16[512,1024]{1,0:T(8,128)(2,1)}, u32[]{:S(2)}) copy-start(bf16[512,1024]{1,0:T(8,128)(2,1)} %get-tuple-element.24) | copy-start | bytes 3145732
  190.4 1.2 copy-start.1
  207.8 26.5 %copy-start.9 = (f32[128]{0:T(128)S(1)}, f32[128]{0:T(128)}, u32[]{:S(2)}) copy-start(f32[128]{0:T(128)} %param.14) | copy-start | bytes 1540
  207.8 26.5 %copy-start.7 = (s32[1,1,128]{2,1,0:T(1,128)S(1)}, s32[1,1,128]{2,1,0:T(1,128)}, u32[]{:S(2)}) copy-start(s32[1,1,128]{2,1,0:T(1,128)} %param.17) | copy-start | bytes 1540
  207.8 26.5 %copy-start.8 = (s32[1,1,128]{2,1,0:T(1,128)S(1)}, s32[1,1,128]{2,1,0:T(1,128)}, u32[]{:S(2)}) copy-start(s32[1,1,128]{2,1,0:T(1,128)} %param.16) | copy-start | bytes 1540
  230.1 20.8 %all-to-all-start.1 = ((bf16[2,8,16,2048]{3,2,0,1:T(8,128)(2,1)}), bf16[2,8,16,2048]{3,2,0,1:T(8,128)(2,1)S(1)}, u32[]{:S(2)}, u32[]{:S(2)}) async-start(bf16[2,8,16,2048]{3,2,0,1:T(8,128)(2,1)} %copy.18), calls=%async_computation.1 | async-start | bytes 2097152 | tf_op jit(solution)/shard_map/all_to_all | solution.py:99
Sparse Core Ops, SparseCore 0:
  13.3 39.6 all-gather.5
  57.1 54.4 all-gather.3
where the time goes:
time: 260 us
  other arithmetic  96.5 us (37%)
  waiting for transfers between devices  66.9 us (26%)
  matrix products  41.4 us (16%)
  blocking collectives  20.8 us (8%)
  local copies, waits for them, and re-layouts  16.5 us (6%)
  between operations  13.6 us (5%)
  starting transfers between devices  4.19 us (2%)
    all_gather x1, waiting for transfers between devices, total_of_pieces(): pieces = lax.all_gather(value, axis).astype(jnp.float32)  39.8 us
    dot_general x5, matrix products, complex_dot(): jnp.dot(jnp.concatenate([left_re, left_im], 0), jnp.concatenate([right_re...  34.8 us
    convert_element_type x1, other arithmetic, body(): moved_re = (second_re * prop_re - second_im * prop_im).astype(jnp.bfloat16)  21 us
    all_to_all x1, blocking collectives, body(): lax.all_to_all(outgoing.reshape(2, row_count, col_count, tile_rows * tile...  20.8 us
    convert_element_type x1, other arithmetic, body(): wave_re = jnp.cos(angle).astype(jnp.bfloat16)  19.4 us
    convert_element_type x1, other arithmetic, body(): forward_re = forward_re.astype(jnp.bfloat16)  18 us
    all_to_all x1, waiting for transfers between devices, body(): lax.all_to_all(lax.all_to_all(outgoing.reshape(2, row_count, col_count, t...  14.9 us
    all_gather x1, waiting for transfers between devices, body(): lax.all_gather(band.astype(jnp.bfloat16), 'row', axis=0, tiled=True)  12.1 us
  transfers between devices with their start and end apart: 3, of which 3 were waited for; matrix products, arithmetic and copies ran while one was open for 17% of the time, Pallas kernels for 0%

commit v1 on v0

v1 whole, which is shorter than its diff:
```python
import functools
import math

import jax
import jax.numpy as jnp
import numpy as np
from jax import lax
from jax.experimental import pallas as pl
from jax.experimental.pallas import tpu as pltpu
from jax.sharding import PartitionSpec as P

N = 1024
WIN = 512
ROWS = 8
COLS = 16
TILT = 16
KINDS = 2 * TILT + 1
TILE_Y = WIN // ROWS
TILE_X = WIN // COLS
BAND_ROWS = N // ROWS
GROUPS = 7
MESH = pl.DeviceIdType.MESH


EDGE = np.concatenate([np.arange(N // 2 - TILT, N // 2), np.arange(-N // 2, -N // 2 + TILT)])


def turn(number, modulus):
    return np.exp(2j * np.pi * np.mod(number, modulus) / modulus)


def fresnel():
    freq = np.arange(-N // 2, N // 2)
    half = np.arange(2 * N)
    return (turn(np.outer(half, freq), 2 * N) * turn(-freq * freq, 4 * N)[None, :]).sum(1) / N


def basis(length):
    table = fresnel()
    place = np.arange(N)
    shift = np.arange(length + TILT)
    apart = 2 * (shift[:, None] - TILT // 2 - place[None, :])
    edge = turn(-EDGE * EDGE, 4 * N)[:, None] * turn(-np.outer(EDGE, place), N) / N
    return np.concatenate([table[np.mod(apart, 2 * N)], table[np.mod(apart + 1, 2 * N)], edge])


def synthesis(length):
    count = length + TILT
    pixel = np.arange(length)
    out = np.zeros((KINDS, length, 2 * count + 2 * TILT), complex)
    for kind in range(KINDS):
        tilt = kind - TILT
        phase = turn(tilt * pixel, N)
        if tilt % 2 == 0:
            place = pixel - tilt // 2 + TILT // 2
        else:
            place = count + pixel - (tilt + 1) // 2 + TILT // 2
        out[kind, pixel, place] = phase
        moved = EDGE + tilt
        flips = ((moved < -N // 2) | (moved >= N // 2)) & (moved % 2 != 0)
        wrapped = -2 * turn((2 * pixel[:, None] - tilt) * EDGE[None, :], 2 * N)
        out[kind, :, 2 * count :] = phase[:, None] * np.where(flips[None, :], wrapped, 0)
    return out


@functools.lru_cache(None)
def tables():
    across = basis(TILE_X).T
    across = np.concatenate([across.real, across.imag], 1)
    across = np.concatenate([across, across], 0)
    down = basis(TILE_Y)
    down = np.concatenate([down.real, down.imag], 0)
    spread_y = synthesis(TILE_Y)
    order = (4 * np.arange(TILE_Y // 4)[None, :] + np.arange(4)[:, None]).reshape(-1)
    spread_y = spread_y[:, order]
    spread_y = np.concatenate([spread_y.real, spread_y.imag], 2).reshape(KINDS * TILE_Y, -1)
    spread_x = synthesis(TILE_X).transpose(0, 2, 1)
    top = np.concatenate([spread_x.real, spread_x.imag], 2)
    bottom = np.concatenate([-spread_x.imag, spread_x.real], 2)
    spread_x = np.concatenate([top, bottom], 1)
    spread_x = np.concatenate([spread_x, spread_x], 2)
    return tuple(
        value.astype(jnp.bfloat16) for value in (across, down, spread_y, spread_x)
    )


@functools.lru_cache(None)
def wave_fit():
    grid = np.cos(np.pi * (np.arange(4000) + 0.5) / 4000) * np.pi
    square = grid * grid
    powers = (square / np.pi**2)[:, None] ** np.arange(8)[None, :]
    even = np.linalg.lstsq(powers, np.cos(grid), rcond=None)[0] / np.pi ** (2 * np.arange(8))
    odd = np.linalg.lstsq(powers, np.sin(grid) / grid, rcond=None)[0] / np.pi ** (2 * np.arange(8))
    return [float(v) for v in even], [float(v) for v in odd]


def cos_sin_reduced(angle):
    even, odd = wave_fit()
    square = angle * angle
    cosine = jnp.full_like(angle, even[-1])
    sine = jnp.full_like(angle, odd[-1])
    for e, o in zip(even[-2::-1], odd[-2::-1]):
        cosine = cosine * square + e
        sine = sine * square + o
    return cosine, sine * angle


TURN_A = 6.28125
TURN_B = 0.0019350051879882812
TURN_C = 2.0 * math.pi - TURN_A - TURN_B


def cos_sin(angle):
    whole = jnp.floor(angle * (0.5 / math.pi) + 0.5)
    return cos_sin_reduced(((angle - whole * TURN_A) - whole * TURN_B) - whole * TURN_C)


def potential_kernel(
    crop,
    atom_y,
    atom_x,
    atom_weight,
    across_hbm,
    down_hbm,
    out,
    prof_x,
    prof_y,
    part,
    landed,
    whole,
    wave,
    across,
    down,
    moved,
    gathered,
    table_sem,
    part_send,
    part_recv,
    whole_send,
    whole_recv,
    moved_send,
    moved_recv,
):
    row = lax.axis_index("row")
    col = lax.axis_index("col")
    barrier = pltpu.get_barrier_semaphore()
    for step in range(1, COLS):
        peer = lax.rem(col + step, COLS)
        pl.semaphore_signal(barrier, inc=1, device_id={"col": peer}, device_id_type=MESH)
    for step in range(1, ROWS):
        peer = lax.rem(row + step, ROWS)
        pl.semaphore_signal(barrier, inc=1, device_id={"row": peer}, device_id_type=MESH)
    start = pl.multiple_of(N - TILE_X * col, TILE_X)
    across_copy = pltpu.make_async_copy(
        across_hbm.at[pl.ds(start, N)], across, table_sem.at[0]
    )
    down_copy = pltpu.make_async_copy(down_hbm, down, table_sem.at[1])
    across_copy.start()
    down_copy.start()

    crop_y = crop[0]
    crop_x = crop[1]
    first_y = (BAND_ROWS * row + crop_y) & (N - 1)
    first_group = ((first_y + (N - 21)) & (N - 1)) // 32
    at_y = ((lax.broadcasted_iota(jnp.int32, (BAND_ROWS, 128), 0) + first_y) & (N - 1)).astype(
        jnp.float32
    )
    lane = lax.broadcasted_iota(jnp.int32, (128, N), 1)
    at_x = ((lane + crop_x) & (N - 1)).astype(jnp.float32)
    for group in range(GROUPS):
        index = (first_group + group) & 31
        here_y = atom_y[pl.ds(index, 1), :]
        here_x = atom_x[pl.ds(index, 1), :]
        here_w = atom_weight[pl.ds(index, 1), :]
        apart = (at_y - here_y) * 0.5
        value = jnp.exp(-(apart * apart)) * here_w
        prof_y[:, 128 * group : 128 * group + 128] = value.astype(jnp.bfloat16)
        column = jnp.transpose(jnp.broadcast_to(here_x, (128, 128)))
        column = jnp.concatenate([column] * (N // 128), axis=1)
        apart = (at_x - column) * 0.5
        prof_x[128 * group : 128 * group + 128, :] = jnp.exp(-(apart * apart)).astype(jnp.bfloat16)
    partial = jnp.dot(prof_y[...], prof_x[...], preferred_element_type=jnp.float32)
    for block in range(COLS):
        high, side = block // 2, block % 2
        part[block] = partial[16 * high : 16 * high + 16, 512 * side : 512 * side + 512].astype(
            jnp.bfloat16
        )
    pl.semaphore_wait(barrier, COLS - 1 + ROWS - 1)

    copies = []
    for step in range(1, COLS):
        peer = lax.rem(col + step, COLS)
        copy = pltpu.make_async_remote_copy(
            src_ref=part.at[peer],
            dst_ref=landed.at[step],
            send_sem=part_send.at[step],
            recv_sem=part_recv.at[step],
            device_id={"col": peer},
            device_id_type=MESH,
        )
        copy.start()
        copies.append(copy)
    total = part[col].astype(jnp.float32)
    for step in range(1, COLS):
        copies[step - 1].wait_recv()
        total = total + landed[step].astype(jnp.float32)
    whole[col] = total.astype(jnp.bfloat16)

    shares = []
    for step in range(1, COLS):
        peer = lax.rem(col + step, COLS)
        share = pltpu.make_async_remote_copy(
            src_ref=whole.at[col],
            dst_ref=whole.at[col],
            send_sem=whole_send.at[step],
            recv_sem=whole_recv.at[step],
            device_id={"col": peer},
            device_id_type=MESH,
        )
        share.start()
        shares.append(share)
    for share in shares:
        share.wait_recv()
    for block in range(COLS):
        high, side = block // 2, block % 2
        real, imag = cos_sin(whole[block].astype(jnp.float32))
        wave[16 * high : 16 * high + 16, 512 * side : 512 * side + 512] = real.astype(jnp.bfloat16)
        wave[
            BAND_ROWS + 16 * high : BAND_ROWS + 16 * high + 16, 512 * side : 512 * side + 512
        ] = imag.astype(jnp.bfloat16)

    across_copy.wait()
    product = jnp.dot(wave[...], across[...], preferred_element_type=jnp.float32)
    real = product[:128, :128] - product[128:, 128:]
    imag = product[:128, 128:] + product[128:, :128]
    both = jnp.concatenate([real, imag], axis=1).astype(jnp.bfloat16)
    moved[0] = both[:64]
    moved[1] = both[64:]
    hops = []
    for step in range(1, ROWS):
        peer = lax.rem(row + step, ROWS)
        for half in range(2):
            hop = pltpu.make_async_remote_copy(
                src_ref=moved.at[half],
                dst_ref=gathered.at[(2 * row + half - peer + 16) & 15],
                send_sem=moved_send.at[2 * step + half],
                recv_sem=moved_recv.at[2 * step + half],
                device_id={"row": peer},
                device_id_type=MESH,
            )
            hop.start()
            hops.append(hop)
    gathered[row] = both[:64]
    gathered[(row + 1) & 15] = both[64:]
    down_copy.wait()
    for hop in hops:
        hop.wait_recv()

    product = jnp.dot(
        down[...], gathered[...].reshape(N, 256), preferred_element_type=jnp.float32
    )
    deep = product.shape[0] // 2
    real = (product[:deep, :128] - product[deep:, 128:]).astype(jnp.bfloat16)
    imag = (product[:deep, 128:] + product[deep:, :128]).astype(jnp.bfloat16)
    out[:deep, :128] = real
    out[:deep, 128:] = imag
    out[deep:, :128] = -imag
    out[deep:, 128:] = real
    for copy in copies + shares + hops:
        copy.wait_send()


def probe_kernel(
    beam_y,
    beam_x,
    core,
    spread_y,
    spread_x,
    tilt_y,
    tilt_x,
    amplitude,
    probe_y,
    probe_x,
    out,
    half,
    field_re,
    field_im,
):
    row = lax.axis_index("row")
    col = lax.axis_index("col")

    middle = core[...]

    def tilts(step, carry):
        rows = pl.ds(pl.multiple_of(step * 192, 192), 192)
        half[rows, :] = jnp.dot(
            spread_y[rows, :], middle, preferred_element_type=jnp.float32
        ).astype(jnp.bfloat16)
        return carry

    lax.fori_loop(0, KINDS * TILE_Y // 192, tilts, 0)

    group = lax.broadcasted_iota(jnp.int32, (16, 128), 1) // 32
    even = (group & 1) == 0

    def one_beam(beam):
        rows = pl.ds(pl.multiple_of((beam_y[beam] + TILT) * TILE_Y, TILE_Y), TILE_Y)
        value = jnp.dot(
            half[rows, :], spread_x[beam_x[beam] + TILT], preferred_element_type=jnp.float32
        )
        a, b, c, d = (value[16 * i : 16 * i + 16] for i in range(4))
        straight = jnp.where(
            group < 2, jnp.where(group == 0, a, b), jnp.where(group == 2, c, d)
        )
        crossed = jnp.where(
            group < 2, jnp.where(group == 0, b, a), jnp.where(group == 2, d, c)
        )
        crossed = jnp.where(even, pltpu.roll(crossed, 96, 1), pltpu.roll(crossed, 32, 1))
        rows = pl.ds(pl.multiple_of(beam * 16, 16), 16)
        field_re[rows, :] = jnp.where(even, straight, crossed)
        field_im[rows, :] = jnp.where(even, crossed, straight)

    def beams(step, carry):
        for inner in range(8):
            one_beam(step * 8 + inner)
        return carry

    lax.fori_loop(0, 16, beams, 0)

    ky = tilt_y[...]
    kx = tilt_x[...]
    at_y = jnp.transpose(jnp.broadcast_to(probe_y[...], (128, 128))) - TILE_Y * row
    at_x = jnp.transpose(jnp.broadcast_to(probe_x[...], (128, 128))) - TILE_X * col
    number = (4 * (ky * at_y + kx * at_x) + ky * ky + kx * kx) & (4 * N - 1)
    number = jnp.where(number >= 2 * N, number - 4 * N, number)
    real, imag = cos_sin_reduced(number.astype(jnp.float32) * (-2.0 * math.pi / (4 * N)))
    weight = amplitude[...] * (1.0 / math.sqrt(128.0))
    coefficient = jnp.concatenate([real * weight, imag * weight], axis=0).astype(jnp.bfloat16)
    for piece in range(16):
        rows = pl.ds(piece, 128, stride=16)
        field = jnp.concatenate([field_re[rows, :], field_im[rows, :]], axis=1)
        field = field.astype(jnp.bfloat16)
        product = jnp.dot(coefficient, field, preferred_element_type=jnp.float32)
        real = product[:128, :128] - product[128:, 128:]
        imag = product[:128, 128:] + product[128:, :128]
        out[:, 128 * piece : 128 * piece + 128] = real * real + imag * imag


def body(
    atom_y, atom_x, atom_weight, beam_ky, beam_kx, beam_amplitude, crop_offset, probe_y, probe_x
):
    across, down, spread_y, spread_x = (jnp.asarray(v) for v in tables())
    vmem = pl.BlockSpec(memory_space=pltpu.VMEM)
    smem = pl.BlockSpec(memory_space=pltpu.SMEM)
    anywhere = pl.BlockSpec(memory_space=pl.ANY)
    bf16 = jnp.bfloat16
    core = pl.pallas_call(
        potential_kernel,
        name="potential_to_basis",
        out_shape=jax.ShapeDtypeStruct((384, 256), bf16),
        in_specs=[smem, vmem, vmem, vmem, anywhere, anywhere],
        out_specs=vmem,
        scratch_shapes=[
            pltpu.VMEM((128 * GROUPS, N), bf16),
            pltpu.VMEM((BAND_ROWS, 128 * GROUPS), bf16),
            pltpu.VMEM((COLS, 16, 512), bf16),
            pltpu.VMEM((COLS, 16, 512), bf16),
            pltpu.VMEM((COLS, 16, 512), bf16),
            pltpu.VMEM((2 * BAND_ROWS, N), bf16),
            pltpu.VMEM((N, 256), bf16),
            pltpu.VMEM((384, N), bf16),
            pltpu.VMEM((2, 64, 256), bf16),
            pltpu.VMEM((16, 64, 256), bf16),
            pltpu.SemaphoreType.DMA((2,)),
            pltpu.SemaphoreType.DMA((COLS,)),
            pltpu.SemaphoreType.DMA((COLS,)),
            pltpu.SemaphoreType.DMA((COLS,)),
            pltpu.SemaphoreType.DMA((COLS,)),
            pltpu.SemaphoreType.DMA((2 * ROWS,)),
            pltpu.SemaphoreType.DMA((2 * ROWS,)),
        ],
        compiler_params=pltpu.CompilerParams(
            collective_id=0, has_side_effects=True, vmem_limit_bytes=24 * 2**20
        ),
    )(
        crop_offset,
        atom_y.reshape(32, 128),
        atom_x.reshape(32, 128),
        atom_weight.reshape(32, 128),
        across,
        down,
    )
    result = pl.pallas_call(
        probe_kernel,
        name="basis_to_probes",
        out_shape=jax.ShapeDtypeStruct((128, 2048), jnp.float32),
        in_specs=[smem, smem] + [vmem] * 8,
        out_specs=vmem,
        scratch_shapes=[
            pltpu.VMEM((KINDS * TILE_Y, 256), bf16),
            pltpu.VMEM((128 * 16, 128), jnp.float32),
            pltpu.VMEM((128 * 16, 128), jnp.float32),
        ],
        compiler_params=pltpu.CompilerParams(vmem_limit_bytes=24 * 2**20),
    )(
        beam_ky,
        beam_kx,
        core,
        spread_y,
        spread_x,
        beam_ky.reshape(1, 128),
        beam_kx.reshape(1, 128),
        beam_amplitude.reshape(1, 128),
        probe_y.reshape(1, 128),
        probe_x.reshape(1, 128),
    )
    return result[None, None]


def solution(mesh):
    return jax.shard_map(
        body,
        mesh=mesh,
        in_specs=(
            P("col"),
            P("col"),
            P("col"),
            P(),
            P(),
            P(),
            P(),
            P("row", "col", None),
            P("row", "col", None),
        ),
        out_specs=P("row", "col", None, None),
        check_vma=False,
    )
```

time: 260 us -> 50.1 us (0.19)
  other arithmetic: 96.5 us -> 0 us
  waiting for transfers between devices: 66.9 us -> 0 us
  matrix products: 41.4 us -> 0 us
  Pallas kernels: 0 us -> 39.4 us
  blocking collectives: 20.8 us -> 0 us
  between operations: 13.6 us -> 0.04 us
  local copies, waits for them, and re-layouts: 16.5 us -> 10.2 us
  starting transfers between devices: 4.19 us -> 0 us
    convert_element_type x10 -> x0, other arithmetic: 86.5 us -> none  [the longest x1 21 us: body(): moved_re = (second_re * prop_re - second_im * prop_im).astype(jnp.bfloat16)]
    all_gather x2 -> x0, waiting for transfers between devices: 51.9 us -> none  [the longest x1 39.8 us: total_of_pieces(): pieces = lax.all_gather(value, axis).astype(jnp.float32)]
    dot_general x6 -> x0, matrix products: 41.4 us -> none  [the longest x5 34.8 us: complex_dot(): jnp.dot(jnp.concatenate([left_re, left_im], 0), jnp.concatenate([right_re...]
    pallas_call x0 -> x2, Pallas kernels: none -> 39.4 us  [the longest x1 29.6 us: body(): pl.pallas_call(potential_kernel, name='potential_to_basis', out_shape=jax...]
    all_to_all x1 -> x0, blocking collectives: 20.8 us -> none  [body(): lax.all_to_all(outgoing.reshape(2, row_count, col_count, tile_rows * tile...]
    all_to_all x1 -> x0, waiting for transfers between devices: 14.9 us -> none  [body(): lax.all_to_all(lax.all_to_all(outgoing.reshape(2, row_count, col_count, t...]
    unnamed x20 -> x26, local copies, waits for them, and re-layouts: 0.5 us -> 10.2 us
    reshape x2 -> x0, local copies, waits for them, and re-layouts: 9.25 us -> none  [body(): outgoing.reshape(2, row_count, col_count, tile_rows * tile_cols)]
  transfers between devices with their start and end apart: 3 -> 0, of which waited for: 3 -> 0; matrix products, arithmetic and copies ran while one was open for 17% -> 0% of each run, Pallas kernels for 0% -> 0%
where the time goes in v1:
time: 50.1 us; the launch traced here: 49.6 us
  Pallas kernels  39.4 us (79%)
  local copies, waits for them, and re-layouts  10.2 us (20%)
    pallas_call x1, Pallas kernels, body(): pl.pallas_call(potential_kernel, name='potential_to_basis', out_shape=jax...  29.6 us
    unnamed x26, local copies, waits for them, and re-layouts  10.2 us
    pallas_call x1, Pallas kernels, body(): pl.pallas_call(probe_kernel, name='basis_to_probes', out_shape=jax.ShapeD...  9.79 us

profile of v1, /device:TPU:0, one launch (start us, length us, event | category | flops | bytes accessed | tf_op | source)
XLA Modules:
  0.0 49.6 jit_solution(7583772831868648963)
XLA Ops:
  0.0 0.0 copy-start.1
  0.0 0.0 copy-start.2
  0.0 1.3 %copy-done.2 = bf16[2048,256]{1,0:T(8,128)(2,1)S(1)} copy-done((bf16[2048,256]{1,0:T(8,128)(2,1)S(1)}, bf16[2048,256]{1,0:T(8,128)(2,1)}, u32[]{:S(2)}) %copy-start.2) | copy-done | bytes 1048600
  1.4 0.0 copy-start.3
  1.4 1.1 %copy-done.3 = bf16[384,1024]{1,0:T(8,128)(2,1)S(1)} copy-done((bf16[384,1024]{1,0:T(8,128)(2,1)S(1)}, bf16[384,1024]{1,0:T(8,128)(2,1)}, u32[]{:S(2)}) %copy-start.3) | copy-done | bytes 786456
  2.5 0.0 copy-start.4
  2.5 0.7 %copy-done.4 = f32[4096]{0:T(1024)S(1)} copy-done((f32[4096]{0:T(1024)S(1)}, f32[4096]{0:T(1024)}, u32[]{:S(2)}) %copy-start.4) | copy-done | bytes 16408
  3.2 0.0 copy-start.5
  3.2 0.7 %copy-done.5 = f32[4096]{0:T(1024)S(1)} copy-done((f32[4096]{0:T(1024)S(1)}, f32[4096]{0:T(1024)}, u32[]{:S(2)}) %copy-start.5) | copy-done | bytes 16408
  3.9 0.0 copy-start.6
  3.9 0.7 %copy-done.6 = f32[4096]{0:T(1024)S(1)} copy-done((f32[4096]{0:T(1024)S(1)}, f32[4096]{0:T(1024)}, u32[]{:S(2)}) %copy-start.6) | copy-done | bytes 16408
  4.6 0.0 copy-start.9
  4.6 0.7 %copy-done.9 = s32[2]{0:T(128)S(1)} copy-done((s32[2]{0:T(128)S(1)}, s32[2]{0:T(128)}, u32[]{:S(2)}) %copy-start.9) | copy-done | bytes 32
  5.3 29.6 %potential_to_basis.1.core = bf16[384,256]{1,0:T(8,128)(2,1)S(1)} custom-call(s32[2]{0:T(128)S(1)} %copy-done.9, f32[32,128]{1,0:T(8,128)S(1)} %bitcast.9, f32[32,128]{1,0:T(8,128)S(1)} %bitcast.10, f32[32,128]{1,0:T(8,128)S(1)} %bitcast.11, bf16[2048,256]{1,0:T(8,128)(2,1)S(1)} %copy-done.2, bf16[384,1024]{1,0:T(8,128)(2,1)S(1)} %copy-done.3), custom_call_target="tpu_custom_call" | custom-call | tf_op jit(solution)/shard_map/potential_to_basis/pallas_call | solution.py:357
  34.9 0.0 copy-done.1
  34.9 0.0 copy-start
  34.9 1.6 %copy-done = bf16[33,256,128]{2,1,0:T(8,128)(2,1)S(1)} copy-done((bf16[33,256,128]{2,1,0:T(8,128)(2,1)S(1)}, bf16[33,256,128]{2,1,0:T(8,128)(2,1)}, u32[]{:S(2)}) %copy-start) | copy-done | bytes 2162712
  36.5 0.0 copy-start.7
  36.5 0.7 %copy-done.7 = s32[128]{0:T(128)S(1)} copy-done((s32[128]{0:T(128)S(1)}, s32[128]{0:T(128)}, u32[]{:S(2)}) %copy-start.7) | copy-done | bytes 536
  37.2 0.0 copy-start.8
  37.2 0.7 %copy-done.8 = s32[128]{0:T(128)S(1)} copy-done((s32[128]{0:T(128)S(1)}, s32[128]{0:T(128)}, u32[]{:S(2)}) %copy-start.8) | copy-done | bytes 536
  37.8 0.0 copy-start.10
  37.8 0.7 %copy-done.10 = f32[128]{0:T(128)S(1)} copy-done((f32[128]{0:T(128)S(1)}, f32[128]{0:T(128)}, u32[]{:S(2)}) %copy-start.10) | copy-done | bytes 536
  38.5 0.0 copy-start.11
  38.5 0.7 %copy-done.11 = s32[1,1,128]{2,1,0:T(1,128)S(1)} copy-done((s32[1,1,128]{2,1,0:T(1,128)S(1)}, s32[1,1,128]{2,1,0:T(1,128)}, u32[]{:S(2)}) %copy-start.11) | copy-done | bytes 536
  39.1 0.0 copy-start.12
  39.1 0.7 %copy-done.12 = s32[1,1,128]{2,1,0:T(1,128)S(1)} copy-done((s32[1,1,128]{2,1,0:T(1,128)S(1)}, s32[1,1,128]{2,1,0:T(1,128)}, u32[]{:S(2)}) %copy-start.12) | copy-done | bytes 536
  39.8 9.8 %basis_to_probes.1 = f32[128,2048]{1,0:T(8,128)} custom-call(s32[128]{0:T(128)S(1)} %copy-done.7, s32[128]{0:T(128)S(1)} %copy-done.8, bf16[384,256]{1,0:T(8,128)(2,1)S(1)} %potential_to_basis.1.core, bf16[2112,384]{1,0:T(8,128)(2,1)S(1)} %copy-done.1, bf16[33,256,128]{2,1,0:T(8,128)(2,1)S(1)} %copy-done, s32[1,128]{1,0:T(1,128)S(1)} %bitcast.12, ...), custom_call_target="tpu_custom_call" | custom-call | tf_op jit(solution)/shard_map/basis_to_probes/pallas_call | solution.py:393
Async XLA Ops:
  0.0 34.9 %copy-start.1 = (bf16[2112,384]{1,0:T(8,128)(2,1)S(1)}, bf16[2112,384]{1,0:T(8,128)(2,1)}, u32[]{:S(2)}) copy-start(bf16[2112,384]{1,0:T(8,128)(2,1)} %constant.10.clone.spread_y) | copy-start | bytes 4866052
  0.0 1.3 %copy-start.2 = (bf16[2048,256]{1,0:T(8,128)(2,1)S(1)}, bf16[2048,256]{1,0:T(8,128)(2,1)}, u32[]{:S(2)}) copy-start(bf16[2048,256]{1,0:T(8,128)(2,1)} %constant.8.clone.across_hbm) | copy-start | bytes 3145732
  1.4 1.1 %copy-start.3 = (bf16[384,1024]{1,0:T(8,128)(2,1)S(1)}, bf16[384,1024]{1,0:T(8,128)(2,1)}, u32[]{:S(2)}) copy-start(bf16[384,1024]{1,0:T(8,128)(2,1)} %constant.9.clone.down_hbm) | copy-start | bytes 2359300
  2.5 0.7 %copy-start.4 = (f32[4096]{0:T(1024)S(1)}, f32[4096]{0:T(1024)}, u32[]{:S(2)}) copy-start(f32[4096]{0:T(1024)} %param.13) | copy-start | bytes 49156
  3.2 0.7 %copy-start.5 = (f32[4096]{0:T(1024)S(1)}, f32[4096]{0:T(1024)}, u32[]{:S(2)}) copy-start(f32[4096]{0:T(1024)} %param.14) | copy-start | bytes 49156
  3.9 0.7 %copy-start.6 = (f32[4096]{0:T(1024)S(1)}, f32[4096]{0:T(1024)}, u32[]{:S(2)}) copy-start(f32[4096]{0:T(1024)} %param.15) | copy-start | bytes 49156
  4.6 0.7 %copy-start.9 = (s32[2]{0:T(128)S(1)}, s32[2]{0:T(128)}, u32[]{:S(2)}) copy-start(s32[2]{0:T(128)} %crop.1) | copy-start | bytes 28
  34.9 1.6 %copy-start = (bf16[33,256,128]{2,1,0:T(8,128)(2,1)S(1)}, bf16[33,256,128]{2,1,0:T(8,128)(2,1)}, u32[]{:S(2)}) copy-start(bf16[33,256,128]{2,1,0:T(8,128)(2,1)} %constant.11.clone.spread_x) | copy-start | bytes 6488068
  36.5 0.7 %copy-start.7 = (s32[128]{0:T(128)S(1)}, s32[128]{0:T(128)}, u32[]{:S(2)}) copy-start(s32[128]{0:T(128)} %beam_y.1) | copy-start | bytes 1540
  37.2 0.7 %copy-start.8 = (s32[128]{0:T(128)S(1)}, s32[128]{0:T(128)}, u32[]{:S(2)}) copy-start(s32[128]{0:T(128)} %beam_x.1) | copy-start | bytes 1540
  37.8 0.7 %copy-start.10 = (f32[128]{0:T(128)S(1)}, f32[128]{0:T(128)}, u32[]{:S(2)}) copy-start(f32[128]{0:T(128)} %param.18) | copy-start | bytes 1540
  38.5 0.7 %copy-start.11 = (s32[1,1,128]{2,1,0:T(1,128)S(1)}, s32[1,1,128]{2,1,0:T(1,128)}, u32[]{:S(2)}) copy-start(s32[1,1,128]{2,1,0:T(1,128)} %param.20) | copy-start | bytes 1540
  39.1 0.7 %copy-start.12 = (s32[1,1,128]{2,1,0:T(1,128)S(1)}, s32[1,1,128]{2,1,0:T(1,128)}, u32[]{:S(2)}) copy-start(s32[1,1,128]{2,1,0:T(1,128)} %param.21) | copy-start | bytes 1540

commit v2 on v1

v2 whole, which is shorter than its diff:
```python
import functools
import math

import jax
import jax.numpy as jnp
import numpy as np
from jax import lax
from jax.experimental import pallas as pl
from jax.experimental.pallas import tpu as pltpu
from jax.sharding import PartitionSpec as P

N = 1024
WIN = 512
ROWS = 8
COLS = 16
TILT = 16
KINDS = 2 * TILT + 1
TILE_Y = WIN // ROWS
TILE_X = WIN // COLS
BAND_ROWS = N // ROWS
GROUPS = 7
CHUNKS = 4
CHUNK_ROWS = BAND_ROWS // CHUNKS
SLICE_HIGH = CHUNK_ROWS // 16
SLICE_WIDE = N * SLICE_HIGH // COLS
PIECE = min(CHUNK_ROWS, TILE_Y)
LEAD = TILE_X * (COLS - 1)
MESH = pl.DeviceIdType.MESH


EDGE = np.concatenate([np.arange(N // 2 - TILT, N // 2), np.arange(-N // 2, -N // 2 + TILT)])


def turn(number, modulus):
    return np.exp(2j * np.pi * np.mod(number, modulus) / modulus)


def fresnel():
    freq = np.arange(-N // 2, N // 2)
    half = np.arange(2 * N)
    return (turn(np.outer(half, freq), 2 * N) * turn(-freq * freq, 4 * N)[None, :]).sum(1) / N


def basis(length):
    table = fresnel()
    place = np.arange(N)
    shift = np.arange(length + TILT)
    apart = 2 * (shift[:, None] - TILT // 2 - place[None, :])
    edge = turn(-EDGE * EDGE, 4 * N)[:, None] * turn(-np.outer(EDGE, place), N) / N
    return np.concatenate([table[np.mod(apart, 2 * N)], table[np.mod(apart + 1, 2 * N)], edge])


def synthesis(length):
    count = length + TILT
    pixel = np.arange(length)
    out = np.zeros((KINDS, length, 2 * count + 2 * TILT), complex)
    for kind in range(KINDS):
        tilt = kind - TILT
        phase = turn(tilt * pixel, N)
        if tilt % 2 == 0:
            place = pixel - tilt // 2 + TILT // 2
        else:
            place = count + pixel - (tilt + 1) // 2 + TILT // 2
        out[kind, pixel, place] = phase
        moved = EDGE + tilt
        flips = ((moved < -N // 2) | (moved >= N // 2)) & (moved % 2 != 0)
        wrapped = -2 * turn((2 * pixel[:, None] - tilt) * EDGE[None, :], 2 * N)
        out[kind, :, 2 * count :] = phase[:, None] * np.where(flips[None, :], wrapped, 0)
    return out


def two_parts(value, axis):
    high = value.astype(jnp.bfloat16).astype(np.float64)
    return np.concatenate([high, value - high], axis)


@functools.lru_cache(None)
def tables():
    across = basis(TILE_X).T
    across = two_parts(np.concatenate([across.real, across.imag], 1), 1)
    across = np.concatenate([across[N - LEAD :], across], 0)
    down = basis(TILE_Y)
    down = two_parts(np.concatenate([down.real, down.imag], 0), 0)
    spread_y = synthesis(TILE_Y)
    order = (4 * np.arange(TILE_Y // 4)[None, :] + np.arange(4)[:, None]).reshape(-1)
    spread_y = spread_y[:, order]
    spread_y = np.concatenate([spread_y.real, spread_y.imag], 2).reshape(KINDS * TILE_Y, -1)
    spread_x = synthesis(TILE_X).transpose(0, 2, 1)
    top = np.concatenate([spread_x.real, spread_x.imag], 2)
    bottom = np.concatenate([-spread_x.imag, spread_x.real], 2)
    spread_x = np.concatenate([top, bottom], 1)
    spread_x = np.concatenate([spread_x, spread_x], 2)
    return tuple(
        value.astype(jnp.bfloat16) for value in (across, down, spread_y, spread_x)
    )


@functools.lru_cache(None)
def wave_fit():
    grid = np.cos(np.pi * (np.arange(4000) + 0.5) / 4000) * np.pi
    square = grid * grid
    powers = (square / np.pi**2)[:, None] ** np.arange(8)[None, :]
    even = np.linalg.lstsq(powers, np.cos(grid), rcond=None)[0] / np.pi ** (2 * np.arange(8))
    odd = np.linalg.lstsq(powers, np.sin(grid) / grid, rcond=None)[0] / np.pi ** (2 * np.arange(8))
    return [float(v) for v in even], [float(v) for v in odd]


def cos_sin_reduced(angle):
    even, odd = wave_fit()
    square = angle * angle
    cosine = jnp.full_like(angle, even[-1])
    sine = jnp.full_like(angle, odd[-1])
    for e, o in zip(even[-2::-1], odd[-2::-1]):
        cosine = cosine * square + e
        sine = sine * square + o
    return cosine, sine * angle


TURN_A = 6.28125
TURN_B = 0.0019350051879882812
TURN_C = 2.0 * math.pi - TURN_A - TURN_B


def cos_sin(angle):
    whole = jnp.floor(angle * (0.5 / math.pi) + 0.5)
    return cos_sin_reduced(((angle - whole * TURN_A) - whole * TURN_B) - whole * TURN_C)


def slice_place(block):
    high, side = block % SLICE_HIGH, block // SLICE_HIGH
    return (
        slice(16 * high, 16 * high + 16),
        slice(SLICE_WIDE * side, SLICE_WIDE * side + SLICE_WIDE),
    )


def potential_kernel(
    crop_hbm,
    atom_y_hbm,
    atom_x_hbm,
    atom_weight_hbm,
    tilt_y_hbm,
    tilt_x_hbm,
    amplitude_hbm,
    probe_y_hbm,
    probe_x_hbm,
    across_hbm,
    down_hbm,
    spread_y_hbm,
    spread_x_hbm,
    core,
    coefficient,
    spread_y,
    spread_x,
    crop,
    atoms,
    beams,
    amplitude,
    prof_x,
    prof_y,
    part,
    landed,
    whole,
    wave,
    across,
    down,
    moved,
    gathered,
    table_sem,
    part_send,
    part_recv,
    whole_send,
    whole_recv,
    moved_send,
    moved_recv,
):
    row = lax.axis_index("row")
    col = lax.axis_index("col")
    start = pl.multiple_of(LEAD - TILE_X * col, TILE_X)
    loads = [
        pltpu.make_async_copy(source, target, table_sem.at[place])
        for place, (source, target) in enumerate(
            (
                (crop_hbm, crop),
                (atom_y_hbm, atoms.at[0]),
                (atom_x_hbm, atoms.at[1]),
                (atom_weight_hbm, atoms.at[2]),
                (tilt_y_hbm, beams.at[0]),
                (tilt_x_hbm, beams.at[1]),
                (probe_y_hbm, beams.at[2]),
                (probe_x_hbm, beams.at[3]),
                (amplitude_hbm, amplitude),
                (across_hbm.at[pl.ds(start, N)], across),
                (down_hbm, down),
                (spread_y_hbm, spread_y),
                (spread_x_hbm, spread_x),
            )
        )
    ]
    for load in loads[:4]:
        load.start()
    barrier = pltpu.get_barrier_semaphore()
    for step in range(1, COLS):
        peer = lax.rem(col + step, COLS)
        pl.semaphore_signal(barrier, inc=1, device_id={"col": peer}, device_id_type=MESH)
    for step in range(1, ROWS):
        peer = lax.rem(row + step, ROWS)
        pl.semaphore_signal(barrier, inc=1, device_id={"row": peer}, device_id_type=MESH)
    for load in loads[4:]:
        load.start()
    for load in loads[:4]:
        load.wait()

    crop_y = crop[0]
    crop_x = crop[1]
    first_y = (BAND_ROWS * row + crop_y) & (N - 1)
    first_group = ((first_y + (N - 21)) & (N - 1)) // 32
    at_y = ((lax.broadcasted_iota(jnp.int32, (BAND_ROWS, 128), 0) + first_y) & (N - 1)).astype(
        jnp.float32
    )
    lane = lax.broadcasted_iota(jnp.int32, (128, N), 1)
    at_x = ((lane + crop_x) & (N - 1)).astype(jnp.float32)
    for group in range(GROUPS):
        index = (first_group + group) & 31
        here_y = atoms[0, pl.ds(index, 1), :]
        here_x = atoms[1, pl.ds(index, 1), :]
        here_w = atoms[2, pl.ds(index, 1), :]
        apart = (at_y - here_y) * 0.5
        value = jnp.exp(-(apart * apart)) * here_w
        prof_y[:, 128 * group : 128 * group + 128] = value.astype(jnp.bfloat16)
        column = jnp.transpose(jnp.broadcast_to(here_x, (128, 128)))
        column = jnp.concatenate([column] * (N // 128), axis=1)
        apart = (at_x - column) * 0.5
        prof_x[128 * group : 128 * group + 128, :] = jnp.exp(-(apart * apart)).astype(jnp.bfloat16)
    partial = jnp.dot(prof_y[...], prof_x[...], preferred_element_type=jnp.float32)
    for chunk in range(CHUNKS):
        rows = partial[CHUNK_ROWS * chunk : CHUNK_ROWS * chunk + CHUNK_ROWS].astype(jnp.bfloat16)
        for block in range(COLS):
            part[chunk, block] = rows[slice_place(block)]
    pl.semaphore_wait(barrier, COLS - 1 + ROWS - 1)

    copies = []
    for chunk in range(CHUNKS):
        for step in range(1, COLS):
            peer = lax.rem(col + step, COLS)
            copy = pltpu.make_async_remote_copy(
                src_ref=part.at[chunk, peer],
                dst_ref=landed.at[chunk, step],
                send_sem=part_send.at[chunk, step],
                recv_sem=part_recv.at[chunk, step],
                device_id={"col": peer},
                device_id_type=MESH,
            )
            copy.start()
            copies.append(copy)

    for load in loads[4:9]:
        load.wait()
    ky = beams[0]
    kx = beams[1]
    at_y = jnp.transpose(jnp.broadcast_to(beams[2], (128, 128))) - TILE_Y * row
    at_x = jnp.transpose(jnp.broadcast_to(beams[3], (128, 128))) - TILE_X * col
    number = (4 * (ky * at_y + kx * at_x) + ky * ky + kx * kx) & (4 * N - 1)
    number = jnp.where(number >= 2 * N, number - 4 * N, number)
    real, imag = cos_sin_reduced(number.astype(jnp.float32) * (-2.0 * math.pi / (4 * N)))
    weight = amplitude[...] * (1.0 / math.sqrt(128.0))
    coefficient[:128] = (real * weight).astype(jnp.bfloat16)
    coefficient[128:] = (imag * weight).astype(jnp.bfloat16)

    shares = []
    for chunk in range(CHUNKS):
        total = part[chunk, col].astype(jnp.float32)
        for step in range(1, COLS):
            copies[(COLS - 1) * chunk + step - 1].wait_recv()
            total = total + landed[chunk, step].astype(jnp.float32)
        whole[chunk, col] = (total - 1.0).astype(jnp.bfloat16)
        for step in range(1, COLS):
            peer = lax.rem(col + step, COLS)
            share = pltpu.make_async_remote_copy(
                src_ref=whole.at[chunk, col],
                dst_ref=whole.at[chunk, col],
                send_sem=whole_send.at[chunk, step],
                recv_sem=whole_recv.at[chunk, step],
                device_id={"col": peer},
                device_id_type=MESH,
            )
            share.start()
            shares.append(share)

    loads[9].wait()
    hops = []
    for chunk in range(CHUNKS):
        for share in shares[(COLS - 1) * chunk : (COLS - 1) * (chunk + 1)]:
            share.wait_recv()
        for block in range(COLS):
            rows, columns = slice_place(block)
            real, imag = cos_sin(whole[chunk, block].astype(jnp.float32) + 1.0)
            wave[rows, columns] = real.astype(jnp.bfloat16)
            wave[slice(CHUNK_ROWS + rows.start, CHUNK_ROWS + rows.stop), columns] = imag.astype(
                jnp.bfloat16
            )
        product = jnp.dot(wave[...], across[...], preferred_element_type=jnp.float32)
        product = product[:, :256] + product[:, 256:]
        real = product[:CHUNK_ROWS, :128] - product[CHUNK_ROWS:, 128:]
        imag = product[:CHUNK_ROWS, 128:] + product[CHUNK_ROWS:, :128]
        both = jnp.concatenate([real, imag], axis=1).astype(jnp.bfloat16)
        pieces = CHUNK_ROWS // PIECE
        for piece in range(pieces):
            number = pieces * chunk + piece
            moved[number] = both[PIECE * piece : PIECE * piece + PIECE]
            for step in range(1, ROWS):
                peer = lax.rem(row + step, ROWS)
                place = row * (BAND_ROWS // PIECE) + number - peer * (TILE_Y // PIECE)
                hop = pltpu.make_async_remote_copy(
                    src_ref=moved.at[number],
                    dst_ref=gathered.at[(place + N) & (N // PIECE - 1)],
                    send_sem=moved_send.at[number, step],
                    recv_sem=moved_recv.at[number, step],
                    device_id={"row": peer},
                    device_id_type=MESH,
                )
                hop.start()
                hops.append(hop)
            place = row * ((BAND_ROWS - TILE_Y) // PIECE) + number
            gathered[place & (N // PIECE - 1)] = both[PIECE * piece : PIECE * piece + PIECE]
    loads[10].wait()
    for hop in hops:
        hop.wait_recv()

    product = jnp.dot(
        down[...], gathered[...].reshape(N, 256), preferred_element_type=jnp.float32
    )
    deep = product.shape[0] // 4
    product = product[: 2 * deep] + product[2 * deep :]
    real = (product[:deep, :128] - product[deep:, 128:]).astype(jnp.bfloat16)
    imag = (product[:deep, 128:] + product[deep:, :128]).astype(jnp.bfloat16)
    core[:deep, :128] = real
    core[:deep, 128:] = imag
    core[deep:, :128] = -imag
    core[deep:, 128:] = real
    for load in loads[11:]:
        load.wait()
    for copy in copies + shares + hops:
        copy.wait_send()


def probe_kernel(
    beam_y_hbm,
    beam_x_hbm,
    core,
    coefficient,
    spread_y,
    spread_x,
    out,
    beam_y,
    beam_x,
    half,
    field_re,
    field_im,
    beam_sem,
):
    loads = [
        pltpu.make_async_copy(beam_y_hbm, beam_y, beam_sem.at[0]),
        pltpu.make_async_copy(beam_x_hbm, beam_x, beam_sem.at[1]),
    ]
    for load in loads:
        load.start()

    middle = core[...]

    def tilts(step, carry):
        rows = pl.ds(pl.multiple_of(step * 192, 192), 192)
        half[rows, :] = jnp.dot(
            spread_y[rows, :], middle, preferred_element_type=jnp.float32
        ).astype(jnp.bfloat16)
        return carry

    lax.fori_loop(0, KINDS * TILE_Y // 192, tilts, 0)

    for load in loads:
        load.wait()
    group = lax.broadcasted_iota(jnp.int32, (16, 128), 1) // 32
    even = (group & 1) == 0

    def one_beam(beam):
        rows = pl.ds(pl.multiple_of((beam_y[beam] + TILT) * TILE_Y, TILE_Y), TILE_Y)
        value = jnp.dot(
            half[rows, :], spread_x[beam_x[beam] + TILT], preferred_element_type=jnp.float32
        )
        a, b, c, d = (value[16 * i : 16 * i + 16] for i in range(4))
        straight = jnp.where(
            group < 2, jnp.where(group == 0, a, b), jnp.where(group == 2, c, d)
        )
        crossed = jnp.where(
            group < 2, jnp.where(group == 0, b, a), jnp.where(group == 2, d, c)
        )
        crossed = jnp.where(even, pltpu.roll(crossed, 96, 1), pltpu.roll(crossed, 32, 1))
        rows = pl.ds(pl.multiple_of(beam * 16, 16), 16)
        field_re[rows, :] = jnp.where(even, straight, crossed)
        field_im[rows, :] = jnp.where(even, crossed, straight)

    def beams(step, carry):
        for inner in range(8):
            one_beam(step * 8 + inner)
        return carry

    lax.fori_loop(0, 16, beams, 0)

    for piece in range(16):
        rows = pl.ds(piece, 128, stride=16)
        field = jnp.concatenate([field_re[rows, :], field_im[rows, :]], axis=1)
        field = field.astype(jnp.bfloat16)
        product = jnp.dot(coefficient[...], field, preferred_element_type=jnp.float32)
        real = product[:128, :128] - product[128:, 128:]
        imag = product[:128, 128:] + product[128:, :128]
        out[:, 128 * piece : 128 * piece + 128] = real * real + imag * imag


def body(
    atom_y, atom_x, atom_weight, beam_ky, beam_kx, beam_amplitude, crop_offset, probe_y, probe_x
):
    across, down, spread_y, spread_x = (jnp.asarray(v) for v in tables())
    vmem = pl.BlockSpec(memory_space=pltpu.VMEM)
    hbm = pl.BlockSpec(memory_space=pltpu.HBM)
    bf16 = jnp.bfloat16
    stay = functools.partial(pltpu.with_memory_space_constraint, memory_space=pltpu.HBM)
    core, coefficient, spread_y, spread_x = pl.pallas_call(
        potential_kernel,
        name="potential_to_basis",
        out_shape=[
            jax.ShapeDtypeStruct((384, 256), bf16),
            jax.ShapeDtypeStruct((256, 128), bf16),
            jax.ShapeDtypeStruct(spread_y.shape, bf16),
            jax.ShapeDtypeStruct(spread_x.shape, bf16),
        ],
        in_specs=[hbm] * 13,
        out_specs=[vmem] * 4,
        scratch_shapes=[
            pltpu.SMEM((2,), jnp.int32),
            pltpu.VMEM((3, 32, 128), jnp.float32),
            pltpu.VMEM((4, 1, 128), jnp.int32),
            pltpu.VMEM((1, 128), jnp.float32),
            pltpu.VMEM((128 * GROUPS, N), bf16),
            pltpu.VMEM((BAND_ROWS, 128 * GROUPS), bf16),
            pltpu.VMEM((CHUNKS, COLS, 16, SLICE_WIDE), bf16),
            pltpu.VMEM((CHUNKS, COLS, 16, SLICE_WIDE), bf16),
            pltpu.VMEM((CHUNKS, COLS, 16, SLICE_WIDE), bf16),
            pltpu.VMEM((2 * CHUNK_ROWS, N), bf16),
            pltpu.VMEM((N, 512), bf16),
            pltpu.VMEM((768, N), bf16),
            pltpu.VMEM((BAND_ROWS // PIECE, PIECE, 256), bf16),
            pltpu.VMEM((N // PIECE, PIECE, 256), bf16),
            pltpu.SemaphoreType.DMA((13,)),
            pltpu.SemaphoreType.DMA((CHUNKS, COLS)),
            pltpu.SemaphoreType.DMA((CHUNKS, COLS)),
            pltpu.SemaphoreType.DMA((CHUNKS, COLS)),
            pltpu.SemaphoreType.DMA((CHUNKS, COLS)),
            pltpu.SemaphoreType.DMA((BAND_ROWS // PIECE, ROWS)),
            pltpu.SemaphoreType.DMA((BAND_ROWS // PIECE, ROWS)),
        ],
        compiler_params=pltpu.CompilerParams(
            collective_id=0, has_side_effects=True, vmem_limit_bytes=24 * 2**20
        ),
    )(
        stay(crop_offset),
        stay(atom_y.reshape(32, 128)),
        stay(atom_x.reshape(32, 128)),
        stay(atom_weight.reshape(32, 128)),
        stay(beam_ky.reshape(1, 128)),
        stay(beam_kx.reshape(1, 128)),
        stay(beam_amplitude.reshape(1, 128)),
        stay(probe_y.reshape(1, 128)),
        stay(probe_x.reshape(1, 128)),
        stay(across),
        stay(down),
        stay(spread_y),
        stay(spread_x),
    )
    result = pl.pallas_call(
        probe_kernel,
        name="basis_to_probes",
        out_shape=jax.ShapeDtypeStruct((128, 2048), jnp.float32),
        in_specs=[hbm] * 2 + [vmem] * 4,
        out_specs=vmem,
        scratch_shapes=[
            pltpu.SMEM((128,), jnp.int32),
            pltpu.SMEM((128,), jnp.int32),
            pltpu.VMEM((KINDS * TILE_Y, 256), bf16),
            pltpu.VMEM((128 * 16, 128), jnp.float32),
            pltpu.VMEM((128 * 16, 128), jnp.float32),
            pltpu.SemaphoreType.DMA((2,)),
        ],
        compiler_params=pltpu.CompilerParams(vmem_limit_bytes=24 * 2**20),
    )(stay(beam_ky), stay(beam_kx), core, coefficient, spread_y, spread_x)
    return result[None, None]


def solution(mesh):
    return jax.shard_map(
        body,
        mesh=mesh,
        in_specs=(
            P("col"),
            P("col"),
            P("col"),
            P(),
            P(),
            P(),
            P(),
            P("row", "col", None),
            P("row", "col", None),
        ),
        out_specs=P("row", "col", None, None),
        check_vma=False,
    )
```

time: 50.1 us -> 38.6 us (0.77)
  local copies, waits for them, and re-layouts: 10.2 us -> 0 us
  Pallas kernels: 39.4 us -> 38.5 us
    unnamed x26 -> x0, local copies, waits for them, and re-layouts: 10.2 us -> none
    pallas_call x1, Pallas kernels: 9.79 us -> 9.07 us  [body(): pl.pallas_call(probe_kernel, name='basis_to_probes', out_shape=jax.ShapeD...]
where the time goes in v2:
time: 38.6 us; the launch traced here: 38.5 us
  Pallas kernels  38.5 us (100%)
    pallas_call x1, Pallas kernels, body(): pl.pallas_call(potential_kernel, name='potential_to_basis', out_shape=[ja...  29.4 us
    pallas_call x1, Pallas kernels, body(): pl.pallas_call(probe_kernel, name='basis_to_probes', out_shape=jax.ShapeD...  9.07 us

profile of v2, /device:TPU:0, one launch (start us, length us, event | category | flops | bytes accessed | tf_op | source)
XLA Modules:
  0.0 38.5 jit_solution(2525929766692750840)
XLA Ops:
  0.0 29.4 %potential_to_basis.1 = (bf16[384,256]{1,0:T(8,128)(2,1)S(1)}, bf16[256,128]{1,0:T(8,128)(2,1)S(1)}, bf16[2112,384]{1,0:T(8,128)(2,1)S(1)}, bf16[33,256,128]{2,1,0:T(8,128)(2,1)S(1)}) custom-call(s32[2]{0:T(128)} %crop_hbm.1, f32[32,128]{1,0:T(8,128)} %bitcast.9, f32[32,128]{1,0:T(8,128)} %bitcast.10, f32[32,128]{1,0:T(8,128)} %bitcast.11, ...), custom_call_target="tpu_custom_call" | custom-call | tf_op jit(solution)/shard_map/potential_to_basis/pallas_call | solution.py:427
  29.4 9.1 %basis_to_probes.1 = f32[128,2048]{1,0:T(8,128)} custom-call(s32[128]{0:T(128)} %beam_y_hbm.1, s32[128]{0:T(128)} %beam_x_hbm.1, bf16[384,256]{1,0:T(8,128)(2,1)S(1)} %get-tuple-element.9.core, bf16[256,128]{1,0:T(8,128)(2,1)S(1)} %get-tuple-element.10.coefficient, bf16[2112,384]{1,0:T(8,128)(2,1)S(1)} %get-tuple-element.11.spread_y, ...), custom_call_target="tpu_custom_call" | custom-call | tf_op jit(solution)/shard_map/basis_to_probes/pallas_call | solution.py:479

commit v3 on v2

--- a/solution.py
+++ b/solution.py
@@ -19,16 +19,17 @@
 TILE_X = WIN // COLS
 BAND_ROWS = N // ROWS
 GROUPS = 7
-CHUNKS = 4
+CHUNKS = 2
+UNROLL = 64
 CHUNK_ROWS = BAND_ROWS // CHUNKS
 SLICE_HIGH = CHUNK_ROWS // 16
 SLICE_WIDE = N * SLICE_HIGH // COLS
-PIECE = min(CHUNK_ROWS, TILE_Y)
 LEAD = TILE_X * (COLS - 1)
 MESH = pl.DeviceIdType.MESH
 
 
 EDGE = np.concatenate([np.arange(N // 2 - TILT, N // 2), np.arange(-N // 2, -N // 2 + TILT)])
+EDGES = (EDGE[EDGE % 2 != 0], EDGE[EDGE % 2 == 0])
 
 
 def turn(number, modulus):
@@ -45,27 +46,28 @@
     table = fresnel()
     place = np.arange(N)
     shift = np.arange(length + TILT)
-    apart = 2 * (shift[:, None] - TILT // 2 - place[None, :])
-    edge = turn(-EDGE * EDGE, 4 * N)[:, None] * turn(-np.outer(EDGE, place), N) / N
-    return np.concatenate([table[np.mod(apart, 2 * N)], table[np.mod(apart + 1, 2 * N)], edge])
+    rows = []
+    for odd in (0, 1):
+        apart = 2 * (shift[:, None] - TILT // 2 - place[None, :]) + odd
+        edge = EDGES[odd]
+        rows.append(table[np.mod(apart, 2 * N)])
+        rows.append(turn(-edge * edge, 4 * N)[:, None] * turn(-np.outer(edge, place), N) / N)
+    return np.concatenate(rows)
 
 
 def synthesis(length):
     count = length + TILT
     pixel = np.arange(length)
-    out = np.zeros((KINDS, length, 2 * count + 2 * TILT), complex)
+    out = np.zeros((KINDS, length, count + TILT), complex)
     for kind in range(KINDS):
         tilt = kind - TILT
+        odd = tilt % 2
         phase = turn(tilt * pixel, N)
-        if tilt % 2 == 0:
-            place = pixel - tilt // 2 + TILT // 2
-        else:
-            place = count + pixel - (tilt + 1) // 2 + TILT // 2
-        out[kind, pixel, place] = phase
-        moved = EDGE + tilt
-        flips = ((moved < -N // 2) | (moved >= N // 2)) & (moved % 2 != 0)
-        wrapped = -2 * turn((2 * pixel[:, None] - tilt) * EDGE[None, :], 2 * N)
-        out[kind, :, 2 * count :] = phase[:, None] * np.where(flips[None, :], wrapped, 0)
+        out[kind, pixel, pixel - (tilt + odd) // 2 + TILT // 2] = phase
+        moved = EDGES[odd] + tilt
+        flips = (moved < -N // 2) | (moved >= N // 2)
+        wrapped = -2 * turn((2 * pixel[:, None] - tilt) * EDGES[odd][None, :], 2 * N)
+        out[kind, :, count:] = phase[:, None] * np.where(flips[None, :], wrapped, 0)
     return out
 
 
@@ -81,9 +83,11 @@
     across = np.concatenate([across[N - LEAD :], across], 0)
     down = basis(TILE_Y)
     down = two_parts(np.concatenate([down.real, down.imag], 0), 0)
+    down = down.reshape(-1, ROWS, 2, TILE_Y).transpose(2, 0, 1, 3)
+    down = down.reshape(2, down.shape[1], ROWS * TILE_Y)
     spread_y = synthesis(TILE_Y)
     order = (4 * np.arange(TILE_Y // 4)[None, :] + np.arange(4)[:, None]).reshape(-1)
-    spread_y = spread_y[:, order]
+    spread_y = np.concatenate([spread_y[0::2], spread_y[1::2]])[:, order]
     spread_y = np.concatenate([spread_y.real, spread_y.imag], 2).reshape(KINDS * TILE_Y, -1)
     spread_x = synthesis(TILE_X).transpose(0, 2, 1)
     top = np.concatenate([spread_x.real, spread_x.imag], 2)
@@ -206,7 +210,7 @@
     for step in range(1, ROWS):
         peer = lax.rem(row + step, ROWS)
         pl.semaphore_signal(barrier, inc=1, device_id={"row": peer}, device_id_type=MESH)
-    for load in loads[4:]:
+    for load in loads[4:9]:
         load.start()
     for load in loads[:4]:
         load.wait()
@@ -254,6 +258,9 @@
             copy.start()
             copies.append(copy)
 
+    for load in loads[9:]:
+        load.start()
+
     for load in loads[4:9]:
         load.wait()
     ky = beams[0]
@@ -304,40 +311,51 @@
         real = product[:CHUNK_ROWS, :128] - product[CHUNK_ROWS:, 128:]
         imag = product[:CHUNK_ROWS, 128:] + product[CHUNK_ROWS:, :128]
         both = jnp.concatenate([real, imag], axis=1).astype(jnp.bfloat16)
-        pieces = CHUNK_ROWS // PIECE
-        for piece in range(pieces):
-            number = pieces * chunk + piece
-            moved[number] = both[PIECE * piece : PIECE * piece + PIECE]
-            for step in range(1, ROWS):
-                peer = lax.rem(row + step, ROWS)
-                place = row * (BAND_ROWS // PIECE) + number - peer * (TILE_Y // PIECE)
-                hop = pltpu.make_async_remote_copy(
-                    src_ref=moved.at[number],
-                    dst_ref=gathered.at[(place + N) & (N // PIECE - 1)],
-                    send_sem=moved_send.at[number, step],
-                    recv_sem=moved_recv.at[number, step],
-                    device_id={"row": peer},
-                    device_id_type=MESH,
-                )
-                hop.start()
-                hops.append(hop)
-            place = row * ((BAND_ROWS - TILE_Y) // PIECE) + number
-            gathered[place & (N // PIECE - 1)] = both[PIECE * piece : PIECE * piece + PIECE]
+        moved[chunk] = both
+        for step in range(1, ROWS):
+            peer = lax.rem(row + step, ROWS)
+            hop = pltpu.make_async_remote_copy(
+                src_ref=moved.at[chunk],
+                dst_ref=gathered.at[chunk, ((2 * row + chunk - peer + 16) & 15) // 2],
+                send_sem=moved_send.at[chunk, step],
+                recv_sem=moved_recv.at[chunk, step],
+                device_id={"row": peer},
+                device_id_type=MESH,
+            )
+            hop.start()
+            hops.append(hop)
+        gathered[chunk, ((row + chunk) & 15) // 2] = both
+
     loads[10].wait()
-    for hop in hops:
-        hop.wait_recv()
-
-    product = jnp.dot(
-        down[...], gathered[...].reshape(N, 256), preferred_element_type=jnp.float32
-    )
+    product = None
+    for chunk in range(CHUNKS):
+        for hop in hops[(ROWS - 1) * chunk : (ROWS - 1) * (chunk + 1)]:
+            hop.wait_recv()
+        term = jnp.dot(
+            down[(row + chunk) & 1],
+            gathered[chunk].reshape(ROWS * TILE_Y, 256),
+            preferred_element_type=jnp.float32,
+        )
+        product = term if product is None else product + term
     deep = product.shape[0] // 4
     product = product[: 2 * deep] + product[2 * deep :]
-    real = (product[:deep, :128] - product[deep:, 128:]).astype(jnp.bfloat16)
-    imag = (product[:deep, 128:] + product[deep:, :128]).astype(jnp.bfloat16)
-    core[:deep, :128] = real
-    core[:deep, 128:] = imag
-    core[deep:, :128] = -imag
-    core[deep:, 128:] = real
+    real = product[:deep, :128] - product[deep:, 128:]
+    imag = product[:deep, 128:] + product[deep:, :128]
+    lower = lax.broadcasted_iota(jnp.int32, (deep, 128), 1) < 64
+    real_turned = pltpu.roll(real, 64, 1)
+    imag_turned = pltpu.roll(imag, 64, 1)
+    rows = deep // 2
+    for side, (first, second) in enumerate(
+        (
+            (jnp.where(lower, real, imag_turned), jnp.where(lower, -imag, real_turned)),
+            (jnp.where(lower, real_turned, imag), jnp.where(lower, -imag_turned, real)),
+        )
+    ):
+        for odd in (0, 1):
+            mine = slice(rows * odd, rows * odd + rows)
+            lanes = slice(128 * side, 128 * side + 128)
+            core[odd, :rows, lanes] = first[mine].astype(jnp.bfloat16)
+            core[odd, rows:, lanes] = second[mine].astype(jnp.bfloat16)
     for load in loads[11:]:
         load.wait()
     for copy in copies + shares + hops:
@@ -357,6 +375,7 @@
     half,
     field_re,
     field_im,
+    result,
     beam_sem,
 ):
     loads = [
@@ -366,16 +385,12 @@
     for load in loads:
         load.start()
 
-    middle = core[...]
-
-    def tilts(step, carry):
-        rows = pl.ds(pl.multiple_of(step * 192, 192), 192)
-        half[rows, :] = jnp.dot(
-            spread_y[rows, :], middle, preferred_element_type=jnp.float32
-        ).astype(jnp.bfloat16)
-        return carry
-
-    lax.fori_loop(0, KINDS * TILE_Y // 192, tilts, 0)
+    middle = (KINDS // 2 + 1) * TILE_Y
+    for odd, rows in enumerate((slice(0, middle), slice(middle, KINDS * TILE_Y))):
+        value = jnp.dot(spread_y[rows], core[odd], preferred_element_type=jnp.float32)
+        value = value.astype(jnp.bfloat16)
+        half[0, rows] = value[:, :128]
+        half[1, rows] = value[:, 128:]
 
     for load in loads:
         load.wait()
@@ -383,9 +398,12 @@
     even = (group & 1) == 0
 
     def one_beam(beam):
-        rows = pl.ds(pl.multiple_of((beam_y[beam] + TILT) * TILE_Y, TILE_Y), TILE_Y)
+        tilt = beam_y[beam]
+        other = beam_x[beam]
+        kind = (tilt & 1) * (KINDS // 2 + 1) + (tilt + TILT) // 2
+        rows = pl.ds(pl.multiple_of(kind * TILE_Y, TILE_Y), TILE_Y)
         value = jnp.dot(
-            half[rows, :], spread_x[beam_x[beam] + TILT], preferred_element_type=jnp.float32
+            half[other & 1, rows, :], spread_x[other + TILT], preferred_element_type=jnp.float32
         )
         a, b, c, d = (value[16 * i : 16 * i + 16] for i in range(4))
         straight = jnp.where(
@@ -400,12 +418,12 @@
         field_im[rows, :] = jnp.where(even, crossed, straight)
 
     def beams(step, carry):
-        for inner in range(8):
-            one_beam(step * 8 + inner)
+        for inner in range(UNROLL):
+            one_beam(step * UNROLL + inner)
         return carry
 
-    lax.fori_loop(0, 16, beams, 0)
-
+    lax.fori_loop(0, 128 // UNROLL, beams, 0)
+    stores = []
     for piece in range(16):
         rows = pl.ds(piece, 128, stride=16)
         field = jnp.concatenate([field_re[rows, :], field_im[rows, :]], axis=1)
@@ -413,7 +431,16 @@
         product = jnp.dot(coefficient[...], field, preferred_element_type=jnp.float32)
         real = product[:128, :128] - product[128:, 128:]
         imag = product[:128, 128:] + product[128:, :128]
-        out[:, 128 * piece : 128 * piece + 128] = real * real + imag * imag
+        result[:, 128 * piece : 128 * piece + 128] = real * real + imag * imag
+        if piece % 4 == 3:
+            lanes = pl.ds(128 * (piece - 3), 512)
+            store = pltpu.make_async_copy(
+                result.at[:, lanes], out.at[:, lanes], beam_sem.at[2 + piece // 4]
+            )
+            store.start()
+            stores.append(store)
+    for store in stores:
+        store.wait()
 
 
 def body(
@@ -428,7 +455,7 @@
         potential_kernel,
         name="potential_to_basis",
         out_shape=[
-            jax.ShapeDtypeStruct((384, 256), bf16),
+            jax.ShapeDtypeStruct((2, 192, 256), bf16),
             jax.ShapeDtypeStruct((256, 128), bf16),
             jax.ShapeDtypeStruct(spread_y.shape, bf16),
             jax.ShapeDtypeStruct(spread_x.shape, bf16),
@@ -447,16 +474,16 @@
             pltpu.VMEM((CHUNKS, COLS, 16, SLICE_WIDE), bf16),
             pltpu.VMEM((2 * CHUNK_ROWS, N), bf16),
             pltpu.VMEM((N, 512), bf16),
-            pltpu.VMEM((768, N), bf16),
-            pltpu.VMEM((BAND_ROWS // PIECE, PIECE, 256), bf16),
-            pltpu.VMEM((N // PIECE, PIECE, 256), bf16),
+            pltpu.VMEM((2, 768, ROWS * TILE_Y), bf16),
+            pltpu.VMEM((CHUNKS, CHUNK_ROWS, 256), bf16),
+            pltpu.VMEM((CHUNKS, ROWS, CHUNK_ROWS, 256), bf16),
             pltpu.SemaphoreType.DMA((13,)),
             pltpu.SemaphoreType.DMA((CHUNKS, COLS)),
             pltpu.SemaphoreType.DMA((CHUNKS, COLS)),
             pltpu.SemaphoreType.DMA((CHUNKS, COLS)),
             pltpu.SemaphoreType.DMA((CHUNKS, COLS)),
-            pltpu.SemaphoreType.DMA((BAND_ROWS // PIECE, ROWS)),
-            pltpu.SemaphoreType.DMA((BAND_ROWS // PIECE, ROWS)),
+            pltpu.SemaphoreType.DMA((CHUNKS, ROWS)),
+            pltpu.SemaphoreType.DMA((CHUNKS, ROWS)),
         ],
         compiler_params=pltpu.CompilerParams(
             collective_id=0, has_side_effects=True, vmem_limit_bytes=24 * 2**20
@@ -481,14 +508,15 @@
         name="basis_to_probes",
         out_shape=jax.ShapeDtypeStruct((128, 2048), jnp.float32),
         in_specs=[hbm] * 2 + [vmem] * 4,
-        out_specs=vmem,
+        out_specs=hbm,
         scratch_shapes=[
             pltpu.SMEM((128,), jnp.int32),
             pltpu.SMEM((128,), jnp.int32),
-            pltpu.VMEM((KINDS * TILE_Y, 256), bf16),
+            pltpu.VMEM((2, KINDS * TILE_Y, 128), bf16),
             pltpu.VMEM((128 * 16, 128), jnp.float32),
             pltpu.VMEM((128 * 16, 128), jnp.float32),
-            pltpu.SemaphoreType.DMA((2,)),
+            pltpu.VMEM((128, 2048), jnp.float32),
+            pltpu.SemaphoreType.DMA((6,)),
         ],
         compiler_params=pltpu.CompilerParams(vmem_limit_bytes=24 * 2**20),
     )(stay(beam_ky), stay(beam_kx), core, coefficient, spread_y, spread_x)

time: 38.6 us -> 33.4 us (0.87)
  Pallas kernels: 38.5 us -> 33.2 us
    pallas_call x1, Pallas kernels: 9.07 us -> 4.5 us  [body(): pl.pallas_call(probe_kernel, name='basis_to_probes', out_shape=jax.ShapeD...]
    pallas_call x1, Pallas kernels: 29.4 us -> 28.7 us  [body(): pl.pallas_call(potential_kernel, name='potential_to_basis', out_shape=[ja...]
where the time goes in v3:
time: 33.4 us; the launch traced here: 33.2 us
  Pallas kernels  33.2 us (99%)
    pallas_call x1, Pallas kernels, body(): pl.pallas_call(potential_kernel, name='potential_to_basis', out_shape=[ja...  28.7 us
    pallas_call x1, Pallas kernels, body(): pl.pallas_call(probe_kernel, name='basis_to_probes', out_shape=jax.ShapeD...  4.5 us

profile of v3, /device:TPU:0, one launch (start us, length us, event | category | flops | bytes accessed | tf_op | source)
XLA Modules:
  0.0 33.2 jit_solution(7094792815155919310)
XLA Ops:
  0.0 28.7 %potential_to_basis.1 = (bf16[2,192,256]{2,1,0:T(8,128)(2,1)S(1)}, bf16[256,128]{1,0:T(8,128)(2,1)S(1)}, bf16[2112,192]{1,0:T(8,128)(2,1)S(1)}, bf16[33,128,128]{2,1,0:T(8,128)(2,1)S(1)}) custom-call(s32[2]{0:T(128)} %crop_hbm.1, f32[32,128]{1,0:T(8,128)} %bitcast.9, f32[32,128]{1,0:T(8,128)} %bitcast.10, f32[32,128]{1,0:T(8,128)} %bitcast.11, ...), custom_call_target="tpu_custom_call" | custom-call | tf_op jit(solution)/shard_map/potential_to_basis/pallas_call | solution.py:454
  28.7 4.5 %basis_to_probes.1 = f32[128,2048]{1,0:T(8,128)} custom-call(s32[128]{0:T(128)} %beam_y_hbm.1, s32[128]{0:T(128)} %beam_x_hbm.1, bf16[2,192,256]{2,1,0:T(8,128)(2,1)S(1)} %get-tuple-element.9.core, bf16[256,128]{1,0:T(8,128)(2,1)S(1)} %get-tuple-element.10.coefficient, bf16[2112,192]{1,0:T(8,128)(2,1)S(1)} %get-tuple-element.11.spread_y, ...), custom_call_target="tpu_custom_call" | custom-call | tf_op jit(solution)/shard_map/basis_to_probes/pallas_call | solution.py:506

commit v4 on v3

--- a/solution.py
+++ b/solution.py
@@ -20,7 +20,7 @@
 BAND_ROWS = N // ROWS
 GROUPS = 7
 CHUNKS = 2
-UNROLL = 64
+UNROLL = 128
 CHUNK_ROWS = BAND_ROWS // CHUNKS
 SLICE_HIGH = CHUNK_ROWS // 16
 SLICE_WIDE = N * SLICE_HIGH // COLS
@@ -156,9 +156,9 @@
     coefficient,
     spread_y,
     spread_x,
+    beams,
     crop,
     atoms,
-    beams,
     amplitude,
     prof_x,
     prof_y,
@@ -363,27 +363,21 @@
 
 
 def probe_kernel(
-    beam_y_hbm,
-    beam_x_hbm,
+    beams,
     core,
     coefficient,
     spread_y,
     spread_x,
     out,
-    beam_y,
-    beam_x,
+    tilts,
     half,
     field_re,
     field_im,
     result,
     beam_sem,
 ):
-    loads = [
-        pltpu.make_async_copy(beam_y_hbm, beam_y, beam_sem.at[0]),
-        pltpu.make_async_copy(beam_x_hbm, beam_x, beam_sem.at[1]),
-    ]
-    for load in loads:
-        load.start()
+    load = pltpu.make_async_copy(beams.at[pl.ds(0, 2)], tilts, beam_sem.at[0])
+    load.start()
 
     middle = (KINDS // 2 + 1) * TILE_Y
     for odd, rows in enumerate((slice(0, middle), slice(middle, KINDS * TILE_Y))):
@@ -392,14 +386,13 @@
         half[0, rows] = value[:, :128]
         half[1, rows] = value[:, 128:]
 
-    for load in loads:
-        load.wait()
+    load.wait()
     group = lax.broadcasted_iota(jnp.int32, (16, 128), 1) // 32
     even = (group & 1) == 0
 
     def one_beam(beam):
-        tilt = beam_y[beam]
-        other = beam_x[beam]
+        tilt = tilts[0, 0, beam]
+        other = tilts[1, 0, beam]
         kind = (tilt & 1) * (KINDS // 2 + 1) + (tilt + TILT) // 2
         rows = pl.ds(pl.multiple_of(kind * TILE_Y, TILE_Y), TILE_Y)
         value = jnp.dot(
@@ -417,12 +410,12 @@
         field_re[rows, :] = jnp.where(even, straight, crossed)
         field_im[rows, :] = jnp.where(even, crossed, straight)
 
-    def beams(step, carry):
+    def some_beams(step, carry):
         for inner in range(UNROLL):
             one_beam(step * UNROLL + inner)
         return carry
 
-    lax.fori_loop(0, 128 // UNROLL, beams, 0)
+    lax.fori_loop(0, 128 // UNROLL, some_beams, 0)
     stores = []
     for piece in range(16):
         rows = pl.ds(piece, 128, stride=16)
@@ -432,10 +425,10 @@
         real = product[:128, :128] - product[128:, 128:]
         imag = product[:128, 128:] + product[128:, :128]
         result[:, 128 * piece : 128 * piece + 128] = real * real + imag * imag
-        if piece % 4 == 3:
-            lanes = pl.ds(128 * (piece - 3), 512)
+        if piece % 2 == 1:
+            lanes = pl.ds(128 * (piece - 1), 256)
             store = pltpu.make_async_copy(
-                result.at[:, lanes], out.at[:, lanes], beam_sem.at[2 + piece // 4]
+                result.at[:, lanes], out.at[:, lanes], beam_sem.at[1 + piece // 2]
             )
             store.start()
             stores.append(store)
@@ -451,7 +444,7 @@
     hbm = pl.BlockSpec(memory_space=pltpu.HBM)
     bf16 = jnp.bfloat16
     stay = functools.partial(pltpu.with_memory_space_constraint, memory_space=pltpu.HBM)
-    core, coefficient, spread_y, spread_x = pl.pallas_call(
+    core, coefficient, spread_y, spread_x, beams = pl.pallas_call(
         potential_kernel,
         name="potential_to_basis",
         out_shape=[
@@ -459,13 +452,13 @@
             jax.ShapeDtypeStruct((256, 128), bf16),
             jax.ShapeDtypeStruct(spread_y.shape, bf16),
             jax.ShapeDtypeStruct(spread_x.shape, bf16),
+            jax.ShapeDtypeStruct((4, 1, 128), jnp.int32),
         ],
         in_specs=[hbm] * 13,
-        out_specs=[vmem] * 4,
+        out_specs=[vmem] * 5,
         scratch_shapes=[
             pltpu.SMEM((2,), jnp.int32),
             pltpu.VMEM((3, 32, 128), jnp.float32),
-            pltpu.VMEM((4, 1, 128), jnp.int32),
             pltpu.VMEM((1, 128), jnp.float32),
             pltpu.VMEM((128 * GROUPS, N), bf16),
             pltpu.VMEM((BAND_ROWS, 128 * GROUPS), bf16),
@@ -507,19 +500,18 @@
         probe_kernel,
         name="basis_to_probes",
         out_shape=jax.ShapeDtypeStruct((128, 2048), jnp.float32),
-        in_specs=[hbm] * 2 + [vmem] * 4,
+        in_specs=[vmem] * 5,
         out_specs=hbm,
         scratch_shapes=[
-            pltpu.SMEM((128,), jnp.int32),
-            pltpu.SMEM((128,), jnp.int32),
+            pltpu.SMEM((2, 1, 128), jnp.int32),
             pltpu.VMEM((2, KINDS * TILE_Y, 128), bf16),
             pltpu.VMEM((128 * 16, 128), jnp.float32),
             pltpu.VMEM((128 * 16, 128), jnp.float32),
             pltpu.VMEM((128, 2048), jnp.float32),
-            pltpu.SemaphoreType.DMA((6,)),
+            pltpu.SemaphoreType.DMA((9,)),
         ],
         compiler_params=pltpu.CompilerParams(vmem_limit_bytes=24 * 2**20),
-    )(stay(beam_ky), stay(beam_kx), core, coefficient, spread_y, spread_x)
+    )(beams, core, coefficient, spread_y, spread_x)
     return result[None, None]
 
 

time: 33.4 us -> 32.8 us (0.982)
  Pallas kernels: 33.2 us -> 32.7 us
    pallas_call x1, Pallas kernels: 4.5 us -> 3.94 us  [body(): pl.pallas_call(probe_kernel, name='basis_to_probes', out_shape=jax.ShapeD...]
where the time goes in v4:
time: 32.8 us; the launch traced here: 32.7 us
  Pallas kernels  32.7 us (100%)
    pallas_call x1, Pallas kernels, body(): pl.pallas_call(potential_kernel, name='potential_to_basis', out_shape=[ja...  28.7 us
    pallas_call x1, Pallas kernels, body(): pl.pallas_call(probe_kernel, name='basis_to_probes', out_shape=jax.ShapeD...  3.94 us

profile of v4, /device:TPU:0, one launch (start us, length us, event | category | flops | bytes accessed | tf_op | source)
XLA Modules:
  0.0 32.7 jit_solution(14333696168345864365)
XLA Ops:
  0.0 28.7 %potential_to_basis.1 = (bf16[2,192,256]{2,1,0:T(8,128)(2,1)S(1)}, bf16[256,128]{1,0:T(8,128)(2,1)S(1)}, bf16[2112,192]{1,0:T(8,128)(2,1)S(1)}, bf16[33,128,128]{2,1,0:T(8,128)(2,1)S(1)}, s32[4,1,128]{2,1,0:T(1,128)S(1)}) custom-call(s32[2]{0:T(128)} %crop_hbm.1, f32[32,128]{1,0:T(8,128)} %bitcast.9, f32[32,128]{1,0:T(8,128)} %bitcast.10, ...), custom_call_target="tpu_custom_call" | custom-call | tf_op jit(solution)/shard_map/potential_to_basis/pallas_call | solution.py:447
  28.7 3.9 %basis_to_probes.1 = f32[128,2048]{1,0:T(8,128)} custom-call(s32[4,1,128]{2,1,0:T(1,128)S(1)} %get-tuple-element.10.beams, bf16[2,192,256]{2,1,0:T(8,128)(2,1)S(1)} %get-tuple-element.11.core, bf16[256,128]{1,0:T(8,128)(2,1)S(1)} %get-tuple-element.12.coefficient, bf16[2112,192]{1,0:T(8,128)(2,1)S(1)} %get-tuple-element.13.spread_y, ...), custom_call_target="tpu_custom_call" | custom-call | tf_op jit(solution)/shard_map/basis_to_probes/pallas_call | solution.py:499

commit v5 on v4

--- a/solution.py
+++ b/solution.py
@@ -246,7 +246,7 @@
     copies = []
     for chunk in range(CHUNKS):
         for step in range(1, COLS):
-            peer = lax.rem(col + step, COLS)
+            peer = lax.rem(col + (COLS - step), COLS)
             copy = pltpu.make_async_remote_copy(
                 src_ref=part.at[chunk, peer],
                 dst_ref=landed.at[chunk, step],
@@ -282,7 +282,7 @@
             total = total + landed[chunk, step].astype(jnp.float32)
         whole[chunk, col] = (total - 1.0).astype(jnp.bfloat16)
         for step in range(1, COLS):
-            peer = lax.rem(col + step, COLS)
+            peer = lax.rem(col + (COLS - step), COLS)
             share = pltpu.make_async_remote_copy(
                 src_ref=whole.at[chunk, col],
                 dst_ref=whole.at[chunk, col],

time: 32.8 us -> 32.4 us (0.988)
  Pallas kernels: 32.7 us -> 32.3 us
    pallas_call x1, Pallas kernels: 28.7 us -> 28.3 us  [body(): pl.pallas_call(potential_kernel, name='potential_to_basis', out_shape=[ja...]
where the time goes in v5:
time: 32.4 us; the launch traced here: 32.3 us
  Pallas kernels  32.3 us (100%)
    pallas_call x1, Pallas kernels, body(): pl.pallas_call(potential_kernel, name='potential_to_basis', out_shape=[ja...  28.3 us
    pallas_call x1, Pallas kernels, body(): pl.pallas_call(probe_kernel, name='basis_to_probes', out_shape=jax.ShapeD...  3.95 us

profile of v5, /device:TPU:0, one launch (start us, length us, event | category | flops | bytes accessed | tf_op | source)
XLA Modules:
  0.0 32.3 jit_solution(889017042868017545)
XLA Ops:
  0.0 28.3 %potential_to_basis.1 = (bf16[2,192,256]{2,1,0:T(8,128)(2,1)S(1)}, bf16[256,128]{1,0:T(8,128)(2,1)S(1)}, bf16[2112,192]{1,0:T(8,128)(2,1)S(1)}, bf16[33,128,128]{2,1,0:T(8,128)(2,1)S(1)}, s32[4,1,128]{2,1,0:T(1,128)S(1)}) custom-call(s32[2]{0:T(128)} %crop_hbm.1, f32[32,128]{1,0:T(8,128)} %bitcast.9, f32[32,128]{1,0:T(8,128)} %bitcast.10, ...), custom_call_target="tpu_custom_call" | custom-call | tf_op jit(solution)/shard_map/potential_to_basis/pallas_call | solution.py:447
  28.3 3.9 %basis_to_probes.1 = f32[128,2048]{1,0:T(8,128)} custom-call(s32[4,1,128]{2,1,0:T(1,128)S(1)} %get-tuple-element.10.beams, bf16[2,192,256]{2,1,0:T(8,128)(2,1)S(1)} %get-tuple-element.11.core, bf16[256,128]{1,0:T(8,128)(2,1)S(1)} %get-tuple-element.12.coefficient, bf16[2112,192]{1,0:T(8,128)(2,1)S(1)} %get-tuple-element.13.spread_y, ...), custom_call_target="tpu_custom_call" | custom-call | tf_op jit(solution)/shard_map/basis_to_probes/pallas_call | solution.py:499
